TPU v7x, 8 devices: a whole 2x2x1 slice. The times are simulated.
8 devices in a mesh: dp: 1 (over z), tp: 8 (over y, x, core).
Axes of the slice: x: 2, y: 2, z: 1, core: 2. Of those that a mesh axis runs over, the one named last changes fastest.
Arguments:
- hidden: bfloat16 [4, 4096, 2048], P('dp', 'tp')
- attn_gain: float32 [2048], replicated
- w_q: bfloat16 [2048, 2048], P(None, 'tp')
- w_k: bfloat16 [2048, 2048], P(None, 'tp')
- w_v: bfloat16 [2048, 2048], P(None, 'tp')
- q_gain: float32 [2048], P('tp')
- k_gain: float32 [2048], P('tp')
- w_o: bfloat16 [2048, 2048], P('tp')
Outputs:
- output 1: bfloat16 [4, 4096, 2048], P('dp', 'tp')
- output 2: bfloat16 [4, 4096, 16, 128], P('dp', None, 'tp')
- output 3: bfloat16 [4, 4096, 16, 128], P('dp', None, 'tp')
All inputs are finite; a program needn't handle non-finite values.
Results may differ from a plain program's by a relative error of at most 0.009045.
Values are sent between devices in bfloat16 or wider.
A program may use at most 1 GiB of HBM per device.

v0:
```python
import jax
import jax.numpy as jnp
from jax import lax
from jax.sharding import PartitionSpec as P

HEAD_DIM = 128


def rope_tables(seq_len, head_dim):
    half_dim = head_dim // 2
    inv_freq = 10000.0 ** (-jnp.arange(half_dim, dtype=jnp.float32) * (2.0 / head_dim))
    angles = jnp.arange(seq_len, dtype=jnp.float32)[:, None] * inv_freq[None, :]
    return jnp.cos(angles), jnp.sin(angles)


def apply_rope(heads_in, cos_tab, sin_tab):
    half_dim = heads_in.shape[-1] // 2
    lower_half = heads_in[..., :half_dim]
    upper_half = heads_in[..., half_dim:]
    cos_bcast = cos_tab[None, :, None, :]
    sin_bcast = sin_tab[None, :, None, :]
    return jnp.concatenate([lower_half * cos_bcast - upper_half * sin_bcast, upper_half * cos_bcast + lower_half * sin_bcast], axis=-1)


def causal_attention(q_rot, k_rot, v_heads):
    seq_len = q_rot.shape[1]
    q_tile = min(seq_len, 128)
    score_scale = q_rot.shape[-1] ** -0.5
    tile_outs = []
    for tile_idx in range(seq_len // q_tile):
        q_start = tile_idx * q_tile
        q_stop = q_start + q_tile
        q_part = q_rot[:, q_start:q_stop]
        if tile_outs:
            q_part, prev_out = lax.optimization_barrier((q_part, tile_outs[-1]))
            tile_outs[-1] = prev_out
        scores = jnp.einsum('bqhd,bkhd->bhqk', q_part, k_rot[:, :q_stop], preferred_element_type=jnp.float32) * score_scale
        q_pos = q_start + jnp.arange(q_tile)
        k_pos = jnp.arange(q_stop)
        scores = jnp.where(q_pos[:, None] >= k_pos[None, :], scores, -1e30)
        prob_bf = jax.nn.softmax(scores, axis=-1).astype(jnp.bfloat16)
        tile_out = jnp.einsum('bhqk,bkhd->bqhd', prob_bf, v_heads[:, :q_stop], preferred_element_type=jnp.float32)
        tile_outs.append(tile_out.astype(jnp.bfloat16))
    return jnp.concatenate(tile_outs, axis=1)


def solution(mesh):
    def local_block(x_local, attn_gain, wq_cols, wk_cols, wv_cols, qg_cols, kg_cols, wo_rows):
        n_batch = x_local.shape[0]
        width = x_local.shape[2]
        x_f32 = x_local.astype(jnp.float32)
        inv_rms = lax.rsqrt(jnp.mean(x_f32 * x_f32, axis=-1, keepdims=True) + 1e-5)
        normed = (x_f32 * inv_rms * attn_gain).astype(jnp.bfloat16)
        h_full = lax.all_gather(normed, 'tp', axis=1, tiled=True)
        seq_len = h_full.shape[1]
        local_cols = wq_cols.shape[1]
        local_heads = local_cols // HEAD_DIM
        q_raw = jnp.einsum('btd,dc->btc', h_full, wq_cols, preferred_element_type=jnp.float32).astype(jnp.bfloat16)
        k_raw = jnp.einsum('btd,dc->btc', h_full, wk_cols, preferred_element_type=jnp.float32).astype(jnp.bfloat16)
        v_raw = jnp.einsum('btd,dc->btc', h_full, wv_cols, preferred_element_type=jnp.float32).astype(jnp.bfloat16)
        part_sq = jnp.stack([jnp.einsum('btc,btc->bt', q_raw, q_raw, preferred_element_type=jnp.float32), jnp.einsum('btc,btc->bt', k_raw, k_raw, preferred_element_type=jnp.float32)])
        total_sq = lax.psum(part_sq, 'tp')
        inv_norm = lax.rsqrt(total_sq / width + 1e-5)
        q_normed = q_raw.astype(jnp.float32) * inv_norm[0][..., None] * qg_cols
        k_normed = k_raw.astype(jnp.float32) * inv_norm[1][..., None] * kg_cols
        cos_tab, sin_tab = rope_tables(seq_len, HEAD_DIM)
        head_shape = (n_batch, seq_len, local_heads, HEAD_DIM)
        q_rot = apply_rope(q_normed.reshape(head_shape), cos_tab, sin_tab).astype(jnp.bfloat16)
        k_rot = apply_rope(k_normed.reshape(head_shape), cos_tab, sin_tab).astype(jnp.bfloat16)
        v_heads = v_raw.reshape(head_shape)
        attn_out = causal_attention(q_rot, k_rot, v_heads).reshape(n_batch, seq_len, local_cols)
        y_part = jnp.einsum('btc,cd->btd', attn_out, wo_rows, preferred_element_type=jnp.float32).astype(jnp.bfloat16)
        y_local = lax.psum_scatter(y_part, 'tp', scatter_dimension=1, tiled=True)
        hidden_out = (x_f32 + y_local.astype(jnp.float32)).astype(jnp.bfloat16)
        return (hidden_out, k_rot, v_heads)

    seq_spec = P('dp', 'tp', None)
    head_spec = P('dp', None, 'tp', None)
    col_spec = P(None, 'tp')
    return jax.shard_map(local_block, mesh=mesh, in_specs=(seq_spec, P(None), col_spec, col_spec, col_spec, P('tp'), P('tp'), P('tp', None)), out_specs=(seq_spec, head_spec, head_spec), check_vma=False)
```

profile of v0, /device:TPU:7, one launch (start us, length us, event | category | flops | bytes accessed | tf_op | source)
XLA Modules:
  0.0 1782.7 jit_solution(18389904740172848126)
XLA Ops:
  59.9 259.0 %all-gather.2.cloned.1.call-done = bf16[4,4096,2048]{2,1,0:T(8,128)(2,1)} async-done(((bf16[4,512,2048]{2,1,0:T(8,128)(2,1)}), bf16[4,4096,2048]{2,1,0:T(8,128)(2,1)}) %all-gather.2.cloned.1.call-update) | async-done | bytes 67108880 | tf_op jit(solution)/shard_map/all_gather | solution.py:54
  319.0 31.3 %fusion.34 = (f32[4,4096]{1,0:T(4,128)S(1)}, bf16[4,4096,256]{1,2,0:T(8,128)(2,1)}) fusion(bf16[4,4096,2048]{2,1,0:T(8,128)(2,1)} %all-gather.2.cloned.1.call-done, bf16[2048,256]{1,0:T(8,128)(2,1)S(1)} %copy-done.82), kind=kOutput, calls=%fused_computation.42 | convolution fusion | flops 17196630016 | bytes 76611584 | tf_op jit(solution)/shard_map/btd,dc->btc/dot_general | solution.py:59
  350.3 31.3 %fusion.33 = (f32[4,4096]{1,0:T(4,128)S(1)}, bf16[4,4096,256]{1,2,0:T(8,128)(2,1)}) fusion(bf16[4,4096,2048]{2,1,0:T(8,128)(2,1)} %all-gather.2.cloned.1.call-done, bf16[2048,256]{1,0:T(8,128)(2,1)S(1)} %copy-done.83), kind=kOutput, calls=%fused_computation.41 | convolution fusion | flops 17196630016 | bytes 76611584 | tf_op jit(solution)/shard_map/btd,dc->btc/dot_general | solution.py:58
  382.4 29.3 %convolution_convert_fusion.1 = bf16[4,4096,256]{1,2,0:T(8,128)(2,1)} fusion(bf16[4,4096,2048]{2,1,0:T(8,128)(2,1)} %all-gather.2.cloned.1.call-done, bf16[2048,256]{1,0:T(8,128)(2,1)} %param.12), kind=kOutput, calls=%fused_computation.153 | convolution fusion | flops 17184063488 | bytes 76546048 | tf_op jit(solution)/shard_map/btd,dc->btc/dot_general | solution.py:60
  423.8 13.1 fusion.32
  454.2 12.2 copy.43
  490.9 12.4 copy.44
  503.2 35.4 %subtract_convert_fusion = (bf16[4,4096,2,64]{3,1,2,0:T(8,128)(2,1)}, bf16[4,4096,2,64]{3,1,2,0:T(8,128)(2,1)}, bf16[4,4096,2,64]{3,1,2,0:T(8,128)(2,1)}, bf16[4,4096,2,64]{3,1,2,0:T(8,128)(2,1)}) fusion(f32[4,4096,2,64]{3,1,2,0:T(8,128)} %copy.45, f32[4,4096,2,64]{3,1,2,0:T(8,128)} %copy.44, f32[4096,64]{1,0:T(8,128)} %get-tuple-element.173, ...), kind=kLoop, calls=%fused_computation.52 | loop fusion | flops 33554432 | bytes 52428800 | tf_op jit(solution)/shard_map/convert
  782.4 12.3 fusion.777
  888.0 15.9 fusion.788
  922.8 16.6 fusion.789
  958.5 17.5 fusion.790
  994.2 16.9 fusion.791
  1086.6 18.3 %fusion.794 = (f32[4,2,128]{2,1,0:T(2,128)S(1)}, f32[4,2,128,3456]{3,2,1,0:T(8,128)}) fusion(f32[4,2,128,3456]{3,2,1,0:T(8,128)} %fusion.96, pred[128,3456]{1,0:T(8,128)(4,1)S(1)} %copy-done.31), kind=kOutput, calls=%fused_computation.842 | output fusion | flops 21237120 | bytes 28758016 | tf_op jit(solution)/shard_map/sub | solution.py:41
  1125.4 19.2 %fusion.795 = (f32[4,2,128]{2,1,0:T(2,128)S(1)}, f32[4,2,128,3584]{3,2,1,0:T(8,128)}) fusion(f32[4,2,128,3584]{3,2,1,0:T(8,128)} %fusion.87, pred[128,3584]{1,0:T(8,128)(4,1)S(1)} %copy-done.30), kind=kOutput, calls=%fused_computation.843 | output fusion | flops 22023680 | bytes 29822976 | tf_op jit(solution)/shard_map/sub | solution.py:41
  1165.5 15.5 fusion.796
  1181.1 19.7 %fusion.420 = bf16[4,128,2,128]{1,3,2,0:T(8,128)(2,1)} fusion(f32[4,2,128]{2,1,0:T(2,128)S(1)} %fusion.796, f32[4,2,128,3712]{3,2,1,0:T(8,128)} %fusion.78, pred[128,3712]{1,0:T(8,128)(4,1)S(1)} %copy-done.29, bf16[4,4096,2,128]{1,3,2,0:T(8,128)(2,1)} %bitcast.199), kind=kOutput, calls=%fused_computation.481 | convolution fusion | flops 999821952 | bytes 39227392 | tf_op jit(solution)/shard_map/bhqk,bkhd->bqhd/dot_general | solution.py:42
  1212.0 20.0 %fusion.797 = (f32[4,2,128]{2,1,0:T(2,128)S(1)}, f32[4,2,128,3840]{3,2,1,0:T(8,128)}) fusion(f32[4,2,128,3840]{3,2,1,0:T(8,128)} %fusion.68, pred[128,3840]{1,0:T(8,128)(4,1)S(1)} %copy-done.28), kind=kOutput, calls=%fused_computation.845 | output fusion | flops 23596800 | bytes 31952896 | tf_op jit(solution)/shard_map/sub | solution.py:41
  1254.1 20.7 %fusion.798 = (f32[4,2,128]{2,1,0:T(2,128)S(1)}, f32[4,2,128,3968]{3,2,1,0:T(8,128)}) fusion(f32[4,2,128,3968]{3,2,1,0:T(8,128)} %fusion.56, pred[128,3968]{1,0:T(8,128)(4,1)S(1)} %copy-done.27), kind=kOutput, calls=%fused_computation.846 | output fusion | flops 24383360 | bytes 33017856 | tf_op jit(solution)/shard_map/sub | solution.py:41
  1338.6 21.2 %fusion.413 = bf16[4,4096,2,128]{1,3,2,0:T(8,128)(2,1)} fusion(bf16[4,4096,2,128]{1,3,2,0:T(8,128)(2,1)} %constant_dynamic-update-slice_fusion, bf16[4,4096,2,128]{1,3,2,0:T(8,128)(2,1)} %bitcast.202, f32[4,2,128]{2,1,0:T(2,128)S(1)} %fusion.799, f32[4,2,128,4096]{3,2,1,0:T(8,128)} %fusion.850, pred[128,4096]{1,0:T(8,128)(4,1)S(1)} %copy-done.26), kind=kOutput, calls=%fused_computation.478 | convolution fusion | flops 1103238144 | bytes 43257856 | tf_op jit(solution)/shard_map/bhqk,bkhd->bqhd/dot_general | solution.py:42
  1359.8 30.1 %convolution_convert_fusion = bf16[4,4096,2048]{2,1,0:T(8,128)(2,1)} fusion(bf16[4,4096,256]{1,2,0:T(8,128)(2,1)} %bitcast.170, bf16[256,2048]{1,0:T(8,128)(2,1)S(1)} %copy-done), kind=kOutput, calls=%fused_computation.32 | convolution fusion | flops 17213423616 | bytes 76546048 | tf_op jit(solution)/shard_map/btc,cd->btd/dot_general | solution.py:72
  1390.0 21.1 %copy.23 = bf16[4,4096,2,128]{3,2,1,0:T(2,128)(2,1)} copy(bf16[4,4096,2,128]{1,3,2,0:T(8,128)(2,1)} %bitcast.203) | data formatting | bytes 16777216
  1411.1 17.5 copy.22
  1428.6 336.8 %reduce-scatter.2.cloned.1.call-done = bf16[4,512,2048]{2,1,0:T(8,128)(2,1)} async-done(((bf16[4,4096,2048]{2,1,0:T(8,128)(2,1)}), bf16[4,512,2048]{2,1,0:T(8,128)(2,1)}) %reduce-scatter.2.cloned.1.call-update) | async-done | bytes 8388624 | tf_op jit(solution)/shard_map/reduce_scatter | solution.py:73
  (424 shorter events, 724.2 us)
Async XLA Ops:
  7.2 1352.7 %copy-start = (bf16[256,2048]{1,0:T(8,128)(2,1)S(1)}, bf16[256,2048]{1,0:T(8,128)(2,1)}, u32[]{:S(2)}) copy-start(bf16[256,2048]{1,0:T(8,128)(2,1)} %param.15) | copy-start | bytes 3145732
  7.2 311.8 %all-gather.2.cloned.1.call-start = ((), (), s32[]{:S(2)}) async-start(), calls=%async_computation.1 | async-start | bytes 75497472 | tf_op jit(solution)/shard_map/all_gather | solution.py:54
  21.2 297.8 %copy-start.82 = (bf16[2048,256]{1,0:T(8,128)(2,1)S(1)}, bf16[2048,256]{1,0:T(8,128)(2,1)}, u32[]{:S(2)}) copy-start(bf16[2048,256]{1,0:T(8,128)(2,1)} %param.11) | copy-start | bytes 3145732
  21.2 401.6 %all-reduce.2.cloned.1.call-start = ((), (), s32[]{:S(2)}) async-start(), calls=%async_computation.2 | async-start | bytes 262144 | tf_op jit(solution)/shard_map/psum | solution.py:62
  59.9 290.4 %copy-start.83 = (bf16[2048,256]{1,0:T(8,128)(2,1)S(1)}, bf16[2048,256]{1,0:T(8,128)(2,1)}, u32[]{:S(2)}) copy-start(bf16[2048,256]{1,0:T(8,128)(2,1)} %param.10) | copy-start | bytes 3145732
  382.3 41.4 %copy-start.80 = (f32[256]{0:T(256)S(1)}, f32[256]{0:T(256)}, u32[]{:S(2)}) copy-start(f32[256]{0:T(256)} %param.13) | copy-start | bytes 3076
  382.3 41.4 %copy-start.81 = (f32[256]{0:T(256)S(1)}, f32[256]{0:T(256)}, u32[]{:S(2)}) copy-start(f32[256]{0:T(256)} %param.14) | copy-start | bytes 3076
  382.4 1383.0 %reduce-scatter.2.cloned.1.call-start = ((), (), s32[]{:S(2)}) async-start(), calls=%async_computation.3 | async-start | bytes 75497472 | tf_op jit(solution)/shard_map/reduce_scatter | solution.py:73
  888.0 24.3 %slice-start.6 = ((s8[8388608]{0:T(1024)(128)(4,1)}), s8[4194304]{0:T(1024)(128)(4,1)S(1)}, s32[]{:S(2)}) async-start(s8[8388608]{0:T(1024)(128)(4,1)} %bitcast.152), calls=%async_computation.10 | async-start | bytes 8388608
  922.8 25.2 %slice-start.8 = ((s8[8388608]{0:T(1024)(128)(4,1)}), s8[4194304]{0:T(1024)(128)(4,1)S(1)}, s32[]{:S(2)}) async-start(s8[8388608]{0:T(1024)(128)(4,1)} %bitcast.154), calls=%async_computation.12 | async-start | bytes 8388608
  994.2 26.0 %slice-start.10 = ((s8[8388608]{0:T(1024)(128)(4,1)}), s8[4194304]{0:T(1024)(128)(4,1)S(1)}, s32[]{:S(2)}) async-start(s8[8388608]{0:T(1024)(128)(4,1)} %bitcast.156), calls=%async_computation.14 | async-start | bytes 8388608
  1306.2 22.4 %copy-start.57 = (bf16[4,128,2,128]{1,3,2,0:T(8,128)(2,1)S(1)}, bf16[4,128,2,128]{1,3,2,0:T(8,128)(2,1)}, u32[]{:S(2)}) copy-start(bf16[4,128,2,128]{1,3,2,0:T(8,128)(2,1)} %fusion.450) | copy-start | bytes 786436
  1306.2 23.2 %copy-start.58 = (bf16[4,128,2,128]{1,3,2,0:T(8,128)(2,1)S(1)}, bf16[4,128,2,128]{1,3,2,0:T(8,128)(2,1)}, u32[]{:S(2)}) copy-start(bf16[4,128,2,128]{1,3,2,0:T(8,128)(2,1)} %fusion.447) | copy-start | bytes 786436
  1306.2 24.0 %copy-start.59 = (bf16[4,128,2,128]{1,3,2,0:T(8,128)(2,1)S(1)}, bf16[4,128,2,128]{1,3,2,0:T(8,128)(2,1)}, u32[]{:S(2)}) copy-start(bf16[4,128,2,128]{1,3,2,0:T(8,128)(2,1)} %fusion.444) | copy-start | bytes 786436
  1306.2 24.8 %copy-start.61 = (bf16[4,128,2,128]{1,3,2,0:T(8,128)(2,1)S(1)}, bf16[4,128,2,128]{1,3,2,0:T(8,128)(2,1)}, u32[]{:S(2)}) copy-start(bf16[4,128,2,128]{1,3,2,0:T(8,128)(2,1)} %fusion.441) | copy-start | bytes 786436
  1306.2 25.5 %copy-start.62 = (bf16[4,128,2,128]{1,3,2,0:T(8,128)(2,1)S(1)}, bf16[4,128,2,128]{1,3,2,0:T(8,128)(2,1)}, u32[]{:S(2)}) copy-start(bf16[4,128,2,128]{1,3,2,0:T(8,128)(2,1)} %fusion.438) | copy-start | bytes 786436
  1306.2 26.3 %copy-start.63 = (bf16[4,128,2,128]{1,3,2,0:T(8,128)(2,1)S(1)}, bf16[4,128,2,128]{1,3,2,0:T(8,128)(2,1)}, u32[]{:S(2)}) copy-start(bf16[4,128,2,128]{1,3,2,0:T(8,128)(2,1)} %fusion.435) | copy-start | bytes 786436
  1306.2 27.0 %copy-start.64 = (bf16[4,128,2,128]{1,3,2,0:T(8,128)(2,1)S(1)}, bf16[4,128,2,128]{1,3,2,0:T(8,128)(2,1)}, u32[]{:S(2)}) copy-start(bf16[4,128,2,128]{1,3,2,0:T(8,128)(2,1)} %fusion.432) | copy-start | bytes 786436
  1306.2 27.8 %copy-start.65 = (bf16[4,128,2,128]{1,3,2,0:T(8,128)(2,1)S(1)}, bf16[4,128,2,128]{1,3,2,0:T(8,128)(2,1)}, u32[]{:S(2)}) copy-start(bf16[4,128,2,128]{1,3,2,0:T(8,128)(2,1)} %fusion.429) | copy-start | bytes 786436
  1306.3 28.5 %copy-start.66 = (bf16[4,128,2,128]{1,3,2,0:T(8,128)(2,1)S(1)}, bf16[4,128,2,128]{1,3,2,0:T(8,128)(2,1)}, u32[]{:S(2)}) copy-start(bf16[4,128,2,128]{1,3,2,0:T(8,128)(2,1)} %fusion.426) | copy-start | bytes 786436
  1306.3 29.3 %copy-start.67 = (bf16[4,128,2,128]{1,3,2,0:T(8,128)(2,1)S(1)}, bf16[4,128,2,128]{1,3,2,0:T(8,128)(2,1)}, u32[]{:S(2)}) copy-start(bf16[4,128,2,128]{1,3,2,0:T(8,128)(2,1)} %fusion.423) | copy-start | bytes 786436
  1306.3 30.0 %copy-start.68 = (bf16[4,128,2,128]{1,3,2,0:T(8,128)(2,1)S(1)}, bf16[4,128,2,128]{1,3,2,0:T(8,128)(2,1)}, u32[]{:S(2)}) copy-start(bf16[4,128,2,128]{1,3,2,0:T(8,128)(2,1)} %fusion.420) | copy-start | bytes 786436
  1306.3 30.8 %copy-start.69 = (bf16[4,128,2,128]{1,3,2,0:T(8,128)(2,1)S(1)}, bf16[4,128,2,128]{1,3,2,0:T(8,128)(2,1)}, u32[]{:S(2)}) copy-start(bf16[4,128,2,128]{1,3,2,0:T(8,128)(2,1)} %fusion.417) | copy-start | bytes 786436
  1306.3 31.5 %copy-start.70 = (bf16[4,128,2,128]{1,3,2,0:T(8,128)(2,1)S(1)}, bf16[4,128,2,128]{1,3,2,0:T(8,128)(2,1)}, u32[]{:S(2)}) copy-start(bf16[4,128,2,128]{1,3,2,0:T(8,128)(2,1)} %fusion.414) | copy-start | bytes 786436
  (85 other events, 693.3 us)
Sparse Core Ops, SparseCore 0:
  21.3 297.6 all-gather.1
  382.5 40.2 all-reduce.1
  1390.1 375.2 reduce-scatter.1
where the time goes:
time: 1800 us; the launch traced here: 1780 us
  matrix products  640 us (36%)
  waiting for transfers between devices  607 us (34%)
  other arithmetic  368 us (20%)
  local copies, waits for them, and re-layouts  153 us (8%)
    reduce_scatter x1, waiting for transfers between devices, local_block(): y_local = lax.psum_scatter(y_part, 'tp', scatter_dimension=1, tiled=True)  337 us
    all_gather x1, waiting for transfers between devices, local_block(): h_full = lax.all_gather(normed, 'tp', axis=1, tiled=True)  259 us
    dot_general x32, matrix products, causal_attention(): jnp.einsum('bhqk,bkhd->bqhd', prob_bf, v_heads[:, :q_stop], preferred_ele...  254 us
    sub x21, other arithmetic, causal_attention(): prob_bf = jax.nn.softmax(scores, axis=-1).astype(jnp.bfloat16)  230 us
    dot_general x29, matrix products, causal_attention(): jnp.einsum('bqhd,bkhd->bhqk', q_part, k_rot[:, :q_stop], preferred_elemen...  196 us
    unnamed x249, local copies, waits for them, and re-layouts  135 us
    sub x11, matrix products, causal_attention(): prob_bf = jax.nn.softmax(scores, axis=-1).astype(jnp.bfloat16)  68.6 us
  transfers between devices with their start and end apart: 3, of which 3 were waited for; matrix products, arithmetic and copies ran while one was open for 6% of the time, Pallas kernels for 0%

commit v1 on v0

v1 whole, which is shorter than its diff:
```python
import functools
import math

import jax
import jax.numpy as jnp
from jax import lax
from jax.experimental import pallas as pl
from jax.experimental.pallas import tpu as pltpu
from jax.sharding import PartitionSpec as P

HEAD_DIM = 128
EPS = 1e-5
MESH = pl.DeviceIdType.MESH


def rope_tables(seq_len):
    half_dim = HEAD_DIM // 2
    inv_freq = 10000.0 ** (-jnp.arange(half_dim, dtype=jnp.float32) * (2.0 / HEAD_DIM))
    angles = jnp.arange(seq_len, dtype=jnp.float32)[:, None] * inv_freq[None, :]
    cos, sin = jnp.cos(angles), jnp.sin(angles)
    return jnp.concatenate([cos, cos], axis=1), jnp.concatenate([-sin, sin], axis=1)


def block_kernel(n, width, h_ref, wq_ref, wk_ref, wv_ref, qg_ref, kg_ref, cos_ref, sin_ref,
                 o_hbm, k_out, v_out,
                 q_s, k_s, vt_s, stats, o_s, st_send, st_recv, o_send, o_recv, o_local):
    step = pl.program_id(0)
    me = lax.axis_index('tp')
    tile = h_ref.shape[0]
    cols = wq_ref.shape[1]
    heads = cols // HEAD_DIM
    groups = tile // HEAD_DIM
    half = n // 2

    def peer(d):
        return {'tp': lax.rem(me + d, n)}

    def stats_copy(chunk, d):
        part = stats.at[me, pl.ds(chunk * half, half)]
        return pltpu.make_async_remote_copy(
            src_ref=part, dst_ref=part, send_sem=st_send.at[d, chunk], recv_sem=st_recv.at[me, chunk],
            device_id=peer(d), device_id_type=MESH)

    def wait_stats(chunk):
        for d in range(1, n):
            src = lax.rem(me + d, n)
            part = stats.at[src, pl.ds(chunk * half, half)]
            pltpu.make_async_remote_copy(
                src_ref=part, dst_ref=part, send_sem=st_send.at[d, chunk], recv_sem=st_recv.at[src, chunk],
                device_id=peer(d), device_id_type=MESH).wait_recv()

    @pl.when(step == 0)
    def _():
        barrier = pltpu.get_barrier_semaphore()
        for d in range(1, n):
            pl.semaphore_signal(barrier, inc=1, device_id=peer(d), device_id_type=MESH)

    @pl.when(step == half)
    def _():
        pl.semaphore_wait(pltpu.get_barrier_semaphore(), n - 1)
        for d in range(1, n):
            stats_copy(0, d).start()

    @pl.when(step < n)
    def _():
        h = h_ref[...]
        q = jnp.dot(h, wq_ref[...], preferred_element_type=jnp.float32).astype(jnp.bfloat16)
        k = jnp.dot(h, wk_ref[...], preferred_element_type=jnp.float32).astype(jnp.bfloat16)
        v = jnp.dot(h, wv_ref[...], preferred_element_type=jnp.float32).astype(jnp.bfloat16)
        q_s[step] = q
        k_s[step] = k
        v_out[...] = v
        vt_s[step] = v.T
        qf, kf = q.astype(jnp.float32), k.astype(jnp.float32)
        q_sq = jnp.sum(qf * qf, axis=1, keepdims=True)
        k_sq = jnp.sum(kf * kf, axis=1, keepdims=True)
        lane = lax.broadcasted_iota(jnp.int32, (HEAD_DIM, HEAD_DIM), 1)
        rows = []
        for g in range(groups):
            part = slice(g * HEAD_DIM, (g + 1) * HEAD_DIM)
            both = jnp.where(lane == 0, q_sq[part], k_sq[part])
            rows.append(both.T[:2])
        stats[me, step] = jnp.concatenate(rows, axis=0)

    @pl.when(step == n)
    def _():
        for d in range(1, n):
            stats_copy(1, d).start()
        wait_stats(0)

    @pl.when(step == n + half)
    def _():
        wait_stats(1)

    @pl.when((step >= n) & (step < 2 * n))
    def _():
        j = step - n
        total = stats[0, j]
        for s in range(1, n):
            total = total + stats[s, j]
        inv = lax.rsqrt(total / width + EPS)
        inv_cols = jnp.concatenate([inv] * (HEAD_DIM // inv.shape[0]), axis=0).T
        for g in range(groups):
            part = slice(g * HEAD_DIM, (g + 1) * HEAD_DIM)
            cos, sin = cos_ref[part, :], sin_ref[part, :]
            for x_s, g_ref, col in ((q_s, qg_ref, 2 * g), (k_s, kg_ref, 2 * g + 1)):
                x = x_s[j, part, :].astype(jnp.float32) * inv_cols[:, col:col + 1] * g_ref[...]
                outs = []
                for hd in range(heads):
                    xh = x[:, hd * HEAD_DIM:(hd + 1) * HEAD_DIM]
                    outs.append((xh * cos + pltpu.roll(xh, HEAD_DIM // 2, 1) * sin).astype(jnp.bfloat16))
                rot = jnp.concatenate(outs, axis=1)
                x_s[j, part, :] = rot
                if x_s is k_s:
                    k_out[part, :] = rot

    def o_copy(d):
        return pltpu.make_async_remote_copy(
            src_ref=o_s.at[d], dst_ref=o_hbm.at[:, pl.ds(pl.multiple_of(me * cols, cols), cols)],
            send_sem=o_send.at[d], recv_sem=o_recv.at[me], device_id=peer(d), device_id_type=MESH)

    def o_own():
        return pltpu.make_async_copy(o_s.at[0], o_hbm.at[:, pl.ds(pl.multiple_of(me * cols, cols), cols)], o_local)

    @pl.when(step >= 2 * n)
    def _():
        d = lax.rem(step - 2 * n + 1, n)
        blk = lax.rem(me + d, n)
        scale = HEAD_DIM ** -0.5 * math.log2(math.e)
        nt = (((1,), (1,)), ((), ()))

        def hcols(hd):
            return slice(hd * HEAD_DIM, (hd + 1) * HEAD_DIM)

        qs = [q_s[blk, :, hcols(hd)] for hd in range(heads)]

        def scores(j, hd):
            return lax.dot_general(k_s[j, :, hcols(hd)], qs[hd], nt, preferred_element_type=jnp.float32)

        key_pos = lax.broadcasted_iota(jnp.int32, (tile, tile), 0)
        query_pos = lax.broadcasted_iota(jnp.int32, (tile, tile), 1)
        keep = key_pos <= query_pos
        carry = []
        for hd in range(heads):
            s = jnp.where(keep, scores(blk, hd), -jnp.inf)
            m = jnp.max(s, axis=0, keepdims=True)
            p = jnp.exp2(s * scale - m * scale)
            l = jnp.sum(p, axis=0, keepdims=True)
            acc = jnp.dot(vt_s[blk, hcols(hd), :], p.astype(jnp.bfloat16), preferred_element_type=jnp.float32)
            carry.append((m, l, acc))

        def body(j, carry):
            out = []
            ss = [scores(j, hd) for hd in range(heads)]
            for hd in range(heads):
                m, l, acc = carry[hd]
                s = ss[hd]
                m_new = jnp.maximum(m, jnp.max(s, axis=0, keepdims=True))
                alpha = jnp.exp2((m - m_new) * scale)
                p = jnp.exp2(s * scale - m_new * scale)
                l = l * alpha + jnp.sum(p, axis=0, keepdims=True)
                acc = acc * alpha + jnp.dot(vt_s[j, hcols(hd), :], p.astype(jnp.bfloat16), preferred_element_type=jnp.float32)
                out.append((m_new, l, acc))
            return tuple(out)

        carry = lax.fori_loop(0, blk, body, tuple(carry))
        for hd in range(heads):
            m, l, acc = carry[hd]
            o_s[d, :, hcols(hd)] = (acc / l).T.astype(jnp.bfloat16)

        @pl.when(d != 0)
        def _():
            o_copy(d).start()

        @pl.when(d == 0)
        def _():
            o_own().start()

    @pl.when(step == 3 * n - 1)
    def _():
        o_own().wait()
        for d in range(1, n):
            src = lax.rem(me + d, n)
            o_copy(d).wait_send()
            pltpu.make_async_remote_copy(
                src_ref=o_s.at[d], dst_ref=o_hbm.at[:, pl.ds(pl.multiple_of(src * cols, cols), cols)],
                send_sem=o_send.at[d], recv_sem=o_recv.at[src], device_id=peer(d), device_id_type=MESH).wait_recv()
            for chunk in range(2):
                stats_copy(chunk, d).wait_send()


def block_call(n, h_full, wq, wk, wv, qg, kg, cos, sin):
    seq, width = h_full.shape
    cols = wq.shape[1]
    tile = seq // n
    heads = cols // HEAD_DIM

    def first(i):
        return (jnp.minimum(i, n - 1), 0)

    def second(i):
        return (jnp.clip(i - n, 0, n - 1), 0)

    def whole(i):
        return (0, 0)

    flops = 2 * seq * width * cols * 3 + 2 * seq * seq * cols * 2
    return pl.pallas_call(
        functools.partial(block_kernel, n, width),
        grid=(3 * n,),
        in_specs=[
            pl.BlockSpec((tile, width), first),
            pl.BlockSpec((width, cols), whole), pl.BlockSpec((width, cols), whole), pl.BlockSpec((width, cols), whole),
            pl.BlockSpec((1, cols), whole), pl.BlockSpec((1, cols), whole),
            pl.BlockSpec((tile, HEAD_DIM), second), pl.BlockSpec((tile, HEAD_DIM), second),
        ],
        out_specs=[
            pl.BlockSpec(memory_space=pl.ANY),
            pl.BlockSpec((tile, cols), second),
            pl.BlockSpec((tile, cols), first),
        ],
        out_shape=[
            jax.ShapeDtypeStruct((tile, n * cols), jnp.bfloat16),
            jax.ShapeDtypeStruct((seq, cols), jnp.bfloat16),
            jax.ShapeDtypeStruct((seq, cols), jnp.bfloat16),
        ],
        scratch_shapes=[
            pltpu.VMEM((n, tile, cols), jnp.bfloat16),
            pltpu.VMEM((n, tile, cols), jnp.bfloat16),
            pltpu.VMEM((n, cols, tile), jnp.bfloat16),
            pltpu.VMEM((n, n, 2 * tile // HEAD_DIM, HEAD_DIM), jnp.float32),
            pltpu.VMEM((n, tile, cols), jnp.bfloat16),
            pltpu.SemaphoreType.DMA((n, 2)),
            pltpu.SemaphoreType.DMA((n, 2)),
            pltpu.SemaphoreType.DMA((n,)),
            pltpu.SemaphoreType.DMA((n,)),
            pltpu.SemaphoreType.DMA,
        ],
        compiler_params=pltpu.CompilerParams(
            collective_id=0, has_side_effects=True, vmem_limit_bytes=52 * 1024 * 1024,
            dimension_semantics=('arbitrary',)),
        cost_estimate=pl.CostEstimate(flops=flops, bytes_accessed=seq * width * 2 + 6 * seq * cols * 2, transcendentals=seq * seq * heads // 2),
        name='attn_block',
    )(h_full, wq, wk, wv, qg, kg, cos, sin)


def solution(mesh):
    n = mesh.shape['tp']

    def local_block(x_local, attn_gain, wq, wk, wv, qg, kg, wo_rows):
        n_batch, rows, width = x_local.shape
        seq = rows * n
        cols = wq.shape[1]
        cos, sin = rope_tables(seq)
        qg2, kg2 = qg.reshape(1, cols), kg.reshape(1, cols)
        gathered = []
        for b in range(n_batch):
            x_f32 = x_local[b].astype(jnp.float32)
            inv_rms = lax.rsqrt(jnp.mean(x_f32 * x_f32, axis=-1, keepdims=True) + EPS)
            normed = (x_f32 * inv_rms * attn_gain).astype(jnp.bfloat16)
            gathered.append(lax.all_gather(normed, 'tp', axis=0, tiled=True))
        wo_src, gathered[-1] = lax.optimization_barrier((wo_rows, gathered[-1]))
        w_o = lax.all_gather(wo_src, 'tp', axis=0, tiled=True)
        os, ks, vs = [], [], []
        for b in range(n_batch):
            o, k, v = block_call(n, gathered[b], wq, wk, wv, qg2, kg2, cos, sin)
            os.append(o)
            ks.append(k)
            vs.append(v)
        o_all = jnp.stack(os)
        y = jnp.einsum('btc,cd->btd', o_all, w_o, preferred_element_type=jnp.float32).astype(jnp.bfloat16)
        hidden_out = (x_local.astype(jnp.float32) + y.astype(jnp.float32)).astype(jnp.bfloat16)
        cache_shape = (n_batch, seq, cols // HEAD_DIM, HEAD_DIM)
        return hidden_out, jnp.stack(ks).reshape(cache_shape), jnp.stack(vs).reshape(cache_shape)

    seq_spec = P('dp', 'tp', None)
    head_spec = P('dp', None, 'tp', None)
    col_spec = P(None, 'tp')
    return jax.shard_map(local_block, mesh=mesh, in_specs=(seq_spec, P(None), col_spec, col_spec, col_spec, P('tp'), P('tp'), P('tp', None)), out_specs=(seq_spec, head_spec, head_spec), check_vma=False)
```

time: 1800 us -> 597 us (0.33)
  matrix products: 640 us -> 25 us
  waiting for transfers between devices: 607 us -> 125 us
  Pallas kernels: 0 us -> 345 us
  other arithmetic: 368 us -> 54.1 us
  local copies, waits for them, and re-layouts: 153 us -> 31.7 us
    dot_general x65 -> x1, matrix products: 572 us -> 25 us  [local_block(): jnp.einsum('btc,cd->btd', o_all, w_o, preferred_element_type=jnp.float32)]
    pallas_call x0 -> x4, Pallas kernels: none -> 345 us  [block_call(): pl.pallas_call(functools.partial(block_kernel, n, width), grid=(3 * n,),...]
    reduce_scatter x1 -> x0, waiting for transfers between devices: 337 us -> none  [local_block(): y_local = lax.psum_scatter(y_part, 'tp', scatter_dimension=1, tiled=True)]
    sub x21 -> x0, other arithmetic: 230 us -> none  [causal_attention(): prob_bf = jax.nn.softmax(scores, axis=-1).astype(jnp.bfloat16)]
    all_gather x1 -> x5, waiting for transfers between devices: 259 us -> 123 us  [the longest x4 123 us: local_block(): gathered.append(lax.all_gather(normed, 'tp', axis=0, tiled=True))]
    unnamed x249 -> x16, local copies, waits for them, and re-layouts: 135 us -> 1.4 us
    sub x11 -> x0, matrix products: 68.6 us -> none  [causal_attention(): prob_bf = jax.nn.softmax(scores, axis=-1).astype(jnp.bfloat16)]
    another operation x0 -> x8, local copies, waits for them, and re-layouts: none -> 30.3 us  [the longest x4 15.9 us: local_block(): jnp.stack(ks).reshape(cache_shape)]
  transfers between devices with their start and end apart: 3 -> 5, of which waited for: 3 -> 4; matrix products, arithmetic and copies ran while one was open for 6% -> 13% of each run, Pallas kernels for 0% -> 58%
where the time goes in v1:
time: 597 us; the launch traced here: 596 us
  Pallas kernels  345 us (58%)
  waiting for transfers between devices  125 us (21%)
  other arithmetic  54.1 us (9%)
  local copies, waits for them, and re-layouts  31.7 us (5%)
  matrix products  25 us (4%)
  between operations  13.9 us (2%)
    pallas_call x4, Pallas kernels, block_call(): pl.pallas_call(functools.partial(block_kernel, n, width), grid=(3 * n,),...  345 us
    all_gather x4, waiting for transfers between devices, local_block(): gathered.append(lax.all_gather(normed, 'tp', axis=0, tiled=True))  123 us
    dot_general x1, matrix products, local_block(): jnp.einsum('btc,cd->btd', o_all, w_o, preferred_element_type=jnp.float32)  25 us
    another operation x1, other arithmetic, local_block(): jnp.stack(ks).reshape(cache_shape)  17.9 us
    another operation x1, other arithmetic, local_block(): jnp.stack(vs).reshape(cache_shape)  16.6 us
    another operation x4, local copies, waits for them, and re-layouts, local_block(): jnp.stack(ks).reshape(cache_shape)  15.9 us
    another operation x4, local copies, waits for them, and re-layouts, local_block(): jnp.stack(vs).reshape(cache_shape)  14.4 us
  transfers between devices with their start and end apart: 5, of which 4 were waited for; matrix products, arithmetic and copies ran while one was open for 13% of the time, Pallas kernels for 58%

profile of v1, /device:TPU:7, one launch (start us, length us, event | category | flops | bytes accessed | tf_op | source)
XLA Modules:
  0.0 595.8 jit_solution(3991255704075962676)
XLA Ops:
  7.2 4.4 fusion.13
  11.7 1.4 copy-done.3
  13.1 4.2 fusion.15
  19.6 7.8 %fusion.27 = (f32[4096,64]{1,0:T(8,128)S(1)}, f32[4096,64]{1,0:T(8,128)S(1)}, f32[4096,64]{1,0:T(8,128)S(1)}) fusion(f32[64]{0:T(128)S(1)} %multiply_power_fusion), kind=kLoop, calls=%fused_computation.37 | loop fusion | flops 524288 | bytes 3145984 | tf_op jit(solution)/shard_map/neg | solution.py:21
  27.4 3.2 pad_maximum_fusion.2
  30.6 71.3 %all-gather.12.cloned.1.call-done.h_ref = bf16[4096,2048]{1,0:T(8,128)(2,1)} async-done(((bf16[512,2048]{1,0:T(8,128)(2,1)}), bf16[4096,2048]{1,0:T(8,128)(2,1)}) %all-gather.12.cloned.1.call-update) | async-done | bytes 16777232 | tf_op jit(solution)/shard_map/all_gather | solution.py:261
  101.9 90.3 %attn_block.7 = (bf16[512,2048]{1,0:T(8,128)(2,1)}, bf16[4096,256]{1,0:T(8,128)(2,1)}, bf16[4096,256]{1,0:T(8,128)(2,1)}) custom-call(bf16[4096,2048]{1,0:T(8,128)(2,1)} %all-gather.12.cloned.1.call-done.h_ref, bf16[2048,256]{1,0:T(8,128)(2,1)S(1)} %copy-done, bf16[2048,256]{1,0:T(8,128)(2,1)} %wk_ref.7, bf16[2048,256]{1,0:T(8,128)(2,1)} %wv_ref.7, ...), custom_call_target="tpu_custom_call" | custom-call | flops 30064771072 | bytes 29360128 | tf_op jit(solution)/shard_map/attn_block/pallas_call | solution.py:208
  192.3 4.0 stack.53
  196.2 2.5 stack.58
  198.8 17.0 %all-gather.10.cloned.1.call-done.h_ref = bf16[4096,2048]{1,0:T(8,128)(2,1)} async-done(((bf16[512,2048]{1,0:T(8,128)(2,1)}), bf16[4096,2048]{1,0:T(8,128)(2,1)}) %all-gather.10.cloned.1.call-update) | async-done | bytes 16777232 | tf_op jit(solution)/shard_map/all_gather | solution.py:261
  215.8 88.8 %attn_block.6 = (bf16[512,2048]{1,0:T(8,128)(2,1)}, bf16[4096,256]{1,0:T(8,128)(2,1)}, bf16[4096,256]{1,0:T(8,128)(2,1)}) custom-call(bf16[4096,2048]{1,0:T(8,128)(2,1)} %all-gather.10.cloned.1.call-done.h_ref, bf16[2048,256]{1,0:T(8,128)(2,1)S(1)} %copy-done, bf16[2048,256]{1,0:T(8,128)(2,1)} %wk_ref.7, bf16[2048,256]{1,0:T(8,128)(2,1)} %wv_ref.7, ...), custom_call_target="tpu_custom_call" | custom-call | flops 30064771072 | bytes 29360128 | tf_op jit(solution)/shard_map/attn_block/pallas_call | solution.py:208
  304.7 4.0 stack.52
  308.6 4.0 stack.57
  312.6 17.7 %all-gather.8.cloned.1.call-done.h_ref = bf16[4096,2048]{1,0:T(8,128)(2,1)} async-done(((bf16[512,2048]{1,0:T(8,128)(2,1)}), bf16[4096,2048]{1,0:T(8,128)(2,1)}) %all-gather.8.cloned.1.call-update) | async-done | bytes 16777232 | tf_op jit(solution)/shard_map/all_gather | solution.py:261
  330.3 88.8 %attn_block.5 = (bf16[512,2048]{1,0:T(8,128)(2,1)}, bf16[4096,256]{1,0:T(8,128)(2,1)}, bf16[4096,256]{1,0:T(8,128)(2,1)}) custom-call(bf16[4096,2048]{1,0:T(8,128)(2,1)} %all-gather.8.cloned.1.call-done.h_ref, bf16[2048,256]{1,0:T(8,128)(2,1)S(1)} %copy-done, bf16[2048,256]{1,0:T(8,128)(2,1)} %wk_ref.7, bf16[2048,256]{1,0:T(8,128)(2,1)} %wv_ref.7, ...), custom_call_target="tpu_custom_call" | custom-call | flops 30064771072 | bytes 29360128 | tf_op jit(solution)/shard_map/attn_block/pallas_call | solution.py:208
  419.1 4.0 stack.51
  423.1 3.9 stack.56
  427.0 17.5 %all-gather.6.cloned.1.call-done.h_ref = bf16[4096,2048]{1,0:T(8,128)(2,1)} async-done(((bf16[512,2048]{1,0:T(8,128)(2,1)}), bf16[4096,2048]{1,0:T(8,128)(2,1)}) %all-gather.6.cloned.1.call-update) | async-done | bytes 16777232 | tf_op jit(solution)/shard_map/all_gather | solution.py:261
  444.5 77.3 %attn_block.4 = (bf16[512,2048]{1,0:T(8,128)(2,1)}, bf16[4096,256]{1,0:T(8,128)(2,1)}, bf16[4096,256]{1,0:T(8,128)(2,1)}) custom-call(bf16[4096,2048]{1,0:T(8,128)(2,1)} %all-gather.6.cloned.1.call-done.h_ref, bf16[2048,256]{1,0:T(8,128)(2,1)S(1)} %copy-done, bf16[2048,256]{1,0:T(8,128)(2,1)} %wk_ref.7, bf16[2048,256]{1,0:T(8,128)(2,1)} %wv_ref.7, ...), custom_call_target="tpu_custom_call" | custom-call | flops 30064771072 | bytes 29360128 | tf_op jit(solution)/shard_map/attn_block/pallas_call | solution.py:208
  521.8 4.0 stack.50
  525.8 4.0 stack.55
  529.8 17.9 %pad_maximum_fusion = bf16[4,4096,2,128]{3,2,1,0:T(2,128)(2,1)} fusion(bf16[1,4096,2,128]{3,2,1,0:T(2,128)(2,1)} %stack.53, bf16[1,4096,2,128]{3,2,1,0:T(2,128)(2,1)} %stack.52, bf16[1,4096,2,128]{3,2,1,0:T(2,128)(2,1)} %stack.51, bf16[1,4096,2,128]{3,2,1,0:T(2,128)(2,1)} %stack.50), kind=kLoop, calls=%fused_computation.9 | loop fusion | flops 12582912 | bytes 16777216 | tf_op jit(solution)/shard_map/stack | solution.py:274
  547.7 16.6 %pad_maximum_fusion.1 = bf16[4,4096,2,128]{3,2,1,0:T(2,128)(2,1)} fusion(bf16[1,4096,2,128]{3,2,1,0:T(2,128)(2,1)S(1)} %stack.58, bf16[1,4096,2,128]{3,2,1,0:T(2,128)(2,1)S(1)} %copy-done.4, bf16[1,4096,2,128]{3,2,1,0:T(2,128)(2,1)S(1)} %copy-done.5, bf16[1,4096,2,128]{3,2,1,0:T(2,128)(2,1)S(1)} %copy-done.6), kind=kLoop, calls=%fused_computation.10 | loop fusion | flops 12582912 | bytes 16777216 | tf_op jit(solution)/shard_map/stack | solution.py:274
  564.2 25.0 %add_convert_fusion = bf16[4,512,2048]{2,1,0:T(8,128)(2,1)} fusion(bf16[4,512,2048]{2,1,0:T(8,128)(2,1)} %param.8, bf16[2048,2048]{1,0:T(8,128)(2,1)} %all-gather.14.cloned.1.call-done, bf16[1,512,2048]{2,1,0:T(8,128)(2,1)} %bitcast.35, bf16[1,512,2048]{2,1,0:T(8,128)(2,1)} %bitcast.36, bf16[1,512,2048]{2,1,0:T(8,128)(2,1)} %bitcast.37, ...), kind=kOutput, calls=%fused_computation | convolution fusion | flops 17213423616 | bytes 33554432 | tf_op jit(solution)/shard_map/btc,cd->btd/dot_general | solution.py:271
  (29 shorter events, 2.4 us)
Async XLA Ops:
  7.2 4.5 copy-start.7
  7.2 94.7 %all-gather.12.cloned.1.call-start = ((), (), s32[]{:S(2)}) async-start(), calls=%async_computation.3 | async-start | bytes 18874368 | tf_op jit(solution)/shard_map/all_gather | solution.py:261
  7.2 5.9 copy-start.3
  17.3 198.6 %all-gather.10.cloned.1.call-start = ((), (), s32[]{:S(2)}) async-start(), calls=%async_computation.2 | async-start | bytes 18874368 | tf_op jit(solution)/shard_map/all_gather | solution.py:261
  18.0 312.3 %all-gather.8.cloned.1.call-start = ((), (), s32[]{:S(2)}) async-start(), calls=%async_computation.1 | async-start | bytes 18874368 | tf_op jit(solution)/shard_map/all_gather | solution.py:261
  18.7 425.8 %all-gather.6.cloned.1.call-start = ((), (), s32[]{:S(2)}) async-start(), calls=%async_computation | async-start | bytes 18874368 | tf_op jit(solution)/shard_map/all_gather | solution.py:261
  19.3 544.9 %all-gather.14.cloned.1.call-start = ((), (), s32[]{:S(2)}) async-start(), calls=%async_computation.4 | async-start | bytes 9437184 | tf_op jit(solution)/shard_map/all_gather | solution.py:263
  27.4 74.5 %copy-start = (bf16[2048,256]{1,0:T(8,128)(2,1)S(1)}, bf16[2048,256]{1,0:T(8,128)(2,1)}, u32[]{:S(2)}) copy-start(bf16[2048,256]{1,0:T(8,128)(2,1)} %wq_ref.7) | copy-start | bytes 3145732
  27.4 74.5 %copy-start.1 = (f32[256]{0:T(256)S(1)}, f32[256]{0:T(256)}, u32[]{:S(2)}) copy-start(f32[256]{0:T(256)} %param.13) | copy-start | bytes 3076
  27.4 74.5 %copy-start.2 = (f32[256]{0:T(256)S(1)}, f32[256]{0:T(256)}, u32[]{:S(2)}) copy-start(f32[256]{0:T(256)} %param.14) | copy-start | bytes 3076
  529.8 17.9 %copy-start.4 = (bf16[1,4096,2,128]{3,2,1,0:T(2,128)(2,1)S(1)}, bf16[1,4096,2,128]{3,2,1,0:T(2,128)(2,1)}, u32[]{:S(2)}) copy-start(bf16[1,4096,2,128]{3,2,1,0:T(2,128)(2,1)} %stack.57) | copy-start | bytes 6291460
  529.8 17.9 %copy-start.5 = (bf16[1,4096,2,128]{3,2,1,0:T(2,128)(2,1)S(1)}, bf16[1,4096,2,128]{3,2,1,0:T(2,128)(2,1)}, u32[]{:S(2)}) copy-start(bf16[1,4096,2,128]{3,2,1,0:T(2,128)(2,1)} %stack.56) | copy-start | bytes 6291460
  529.8 17.9 %copy-start.6 = (bf16[1,4096,2,128]{3,2,1,0:T(2,128)(2,1)S(1)}, bf16[1,4096,2,128]{3,2,1,0:T(2,128)(2,1)}, u32[]{:S(2)}) copy-start(bf16[1,4096,2,128]{3,2,1,0:T(2,128)(2,1)} %stack.55) | copy-start | bytes 6291460
Sparse Core Ops, SparseCore 0:
  17.4 84.4 all-gather.11
  104.3 111.4 all-gather.9
  218.2 112.0 all-gather.7
  332.5 111.9 all-gather.5
  446.2 62.4 all-gather.13

commit v2 on v1

--- a/solution.py
+++ b/solution.py
@@ -13,17 +13,208 @@
 MESH = pl.DeviceIdType.MESH
 
 
-def rope_tables(seq_len):
-    half_dim = HEAD_DIM // 2
-    inv_freq = 10000.0 ** (-jnp.arange(half_dim, dtype=jnp.float32) * (2.0 / HEAD_DIM))
-    angles = jnp.arange(seq_len, dtype=jnp.float32)[:, None] * inv_freq[None, :]
-    cos, sin = jnp.cos(angles), jnp.sin(angles)
-    return jnp.concatenate([cos, cos], axis=1), jnp.concatenate([-sin, sin], axis=1)
-
-
-def block_kernel(n, width, h_ref, wq_ref, wk_ref, wv_ref, qg_ref, kg_ref, cos_ref, sin_ref,
-                 o_hbm, k_out, v_out,
-                 q_s, k_s, vt_s, stats, o_s, st_send, st_recv, o_send, o_recv, o_local):
+FIRST = ((0, 2), (2, 1), (3, 1), (4, 4))
+SECOND = ((4, 2), (6, 1), (7, 1), (0, 4))
+PIECES = FIRST + SECOND + ((4, 4), (0, 4))
+LAST = len(PIECES)
+
+
+class RingGather:
+    def __init__(self, buf, own, stage, me, ici_send, ici_recv, d2d_send, d2d_recv, keep):
+        self.buf, self.own, self.stage, self.me, self.rows = buf, own, stage, me, own.shape[0]
+        self.ici_send, self.ici_recv, self.d2d_send, self.d2d_recv, self.keep = ici_send, ici_recv, d2d_send, d2d_recv, keep
+        self.xn = me + 2 - 4 * lax.rem(me // 2, 2)
+        self.yn = me + 4 - 8 * (me // 4)
+        self.dg = self.yn + 2 - 4 * lax.rem(me // 2, 2)
+        self.pt = me + 1 - 2 * lax.rem(me, 2)
+
+    def block(self, block):
+        return self.buf.at[pl.ds(pl.multiple_of(block * self.rows, self.rows), self.rows)]
+
+    def span(self, piece):
+        unit = self.rows // 8
+        return PIECES[piece][0] * unit, PIECES[piece][1] * unit
+
+    def slot(self, block, piece):
+        first, rows = self.span(piece)
+        unit = self.rows // 8
+        return self.buf.at[pl.ds(pl.multiple_of(block * self.rows + first, unit), rows)]
+
+    def staged(self, piece):
+        first, rows = self.span(piece)
+        which = 0 if piece < 4 else 1 if piece < 8 else 2
+        return self.stage.at[which, pl.ds(first, rows)]
+
+    def source(self, piece):
+        return self.xn if piece < 4 else self.yn if piece < 8 else self.dg
+
+    def copy(self, piece):
+        first, rows = self.span(piece)
+        if piece < 8:
+            src = self.own.at[pl.ds(first, rows)]
+        else:
+            src = self.stage.at[1 if piece == 8 else 0, pl.ds(first, rows)]
+        return pltpu.make_async_remote_copy(
+            src_ref=src, dst_ref=self.staged(piece), send_sem=self.ici_send.at[piece], recv_sem=self.ici_recv.at[piece],
+            device_id={'tp': self.xn if piece < 4 or piece == 8 else self.yn}, device_id_type=MESH)
+
+    def handover(self, piece):
+        if piece == LAST:
+            src, dst = self.own, self.block(self.me)
+        else:
+            src, dst = self.staged(piece), self.slot(self.source(piece), piece)
+        return pltpu.make_async_remote_copy(
+            src_ref=src, dst_ref=dst, send_sem=self.d2d_send.at[piece], recv_sem=self.d2d_recv.at[piece],
+            device_id={'tp': self.pt}, device_id_type=MESH)
+
+    def store(self, piece):
+        return pltpu.make_async_copy(self.staged(piece), self.slot(self.source(piece), piece), self.keep.at[piece])
+
+    def send(self, turns):
+        for turn in turns:
+            self.copy(turn).start()
+            self.copy(4 + turn).start()
+        if 3 in turns:
+            self.handover(LAST).start()
+
+    def relay(self):
+        for turns, onward in (((0, 1, 2), 9), ((4, 5, 6), 8)):
+            for piece in turns:
+                self.copy(piece).wait_recv()
+            self.copy(onward).start()
+        self.pass_on((0, 1, 2, 4, 5, 6))
+
+    def pass_on(self, pieces):
+        for piece in pieces:
+            self.handover(piece).start()
+            self.store(piece).start()
+
+    def take(self, pieces):
+        for piece in pieces:
+            self.copy(piece).wait_recv()
+            self.pass_on((piece,))
+
+    def finish(self):
+        self.take((8, 9))
+        for piece in range(LAST):
+            self.copy(piece).wait_send()
+            self.store(piece).wait()
+        for piece in range(LAST + 1):
+            src = self.pt if piece == LAST else self.pt + self.source(piece) - self.me
+            part = self.block(src) if piece == LAST else self.slot(src, piece)
+            pltpu.make_async_remote_copy(
+                src_ref=part, dst_ref=part, send_sem=self.d2d_send.at[piece], recv_sem=self.d2d_recv.at[piece],
+                device_id={'tp': self.pt}, device_id_type=MESH).wait_recv()
+            self.handover(piece).wait_send()
+
+
+GATHER_SEMS = [pltpu.SemaphoreType.DMA((LAST,)), pltpu.SemaphoreType.DMA((LAST,)),
+               pltpu.SemaphoreType.DMA((LAST + 1,)), pltpu.SemaphoreType.DMA((LAST + 1,)), pltpu.SemaphoreType.DMA((LAST,))]
+
+
+def greet(n, me):
+    barrier = pltpu.get_barrier_semaphore()
+    for d in range(1, n):
+        pl.semaphore_signal(barrier, inc=1, device_id={'tp': lax.rem(me + d, n)}, device_id_type=MESH)
+
+
+def first_kernel(n, n_batch, x_hbm, gain_ref, wo_hbm, freq_ref,
+                 h0, h1, h2, h3, wo_full, cos_hbm, sin_hbm,
+                 x_v, h_v, wo_v, stage, cos_v, sin_v, in_sem, wo_sem, out_sem, tab_sem, *gather_sems):
+    me = lax.axis_index('tp')
+    rows, width = x_v.shape[1:]
+    wo_rows = wo_v.shape[0]
+    hs = (h0, h1, h2, h3)
+    greet(n, me)
+    loads = [pltpu.make_async_copy(x_hbm.at[b], x_v.at[b], in_sem.at[b]) for b in range(n_batch)]
+    wo_load = pltpu.make_async_copy(wo_hbm, wo_v, wo_sem.at[0])
+    wo_store = pltpu.make_async_copy(wo_v, wo_full.at[pl.ds(pl.multiple_of(me * wo_rows, wo_rows), wo_rows)], wo_sem.at[1])
+    stores = [pltpu.make_async_copy(h_v.at[b], hs[b].at[pl.ds(pl.multiple_of(me * rows, rows), rows)], out_sem.at[b])
+              for b in range(n_batch)]
+    loads[0].start()
+
+    def norm(b):
+        def body(r, carry):
+            part = pl.ds(pl.multiple_of(r * 64, 64), 64)
+            x = x_v[b, part, :].astype(jnp.float32)
+            inv = lax.rsqrt(jnp.mean(x * x, axis=-1, keepdims=True) + EPS)
+            h_v[b, part, :] = (x * inv * gain_ref[...]).astype(jnp.bfloat16)
+            return carry
+        lax.fori_loop(0, rows // 64, body, 0)
+
+    loads[0].wait()
+    for load in loads[1:]:
+        load.start()
+    wo_load.start()
+    norm(0)
+    pl.semaphore_wait(pltpu.get_barrier_semaphore(), n - 1)
+    gather = RingGather(h0, h_v.at[0], stage, me, *gather_sems)
+    gather.send((0, 1, 2, 3))
+    stores[0].start()
+    for b in range(1, n_batch):
+        loads[b].wait()
+        norm(b)
+        stores[b].start()
+    wo_load.wait()
+    wo_store.start()
+    seq = cos_v.shape[0]
+
+    def table(r, carry):
+        part = pl.ds(pl.multiple_of(r * 64, 64), 64)
+        pos = (lax.broadcasted_iota(jnp.int32, (64, HEAD_DIM), 0) + r * 64).astype(jnp.float32)
+        lane = lax.broadcasted_iota(jnp.int32, (64, HEAD_DIM), 1)
+        angle = pos * freq_ref[...]
+        sin = jnp.sin(angle)
+        cos_v[part, :] = jnp.cos(angle)
+        sin_v[part, :] = jnp.where(lane < HEAD_DIM // 2, -sin, sin)
+        return carry
+
+    lax.fori_loop(0, seq // 64, table, 0)
+    tables = [pltpu.make_async_copy(cos_v, cos_hbm, tab_sem.at[0]), pltpu.make_async_copy(sin_v, sin_hbm, tab_sem.at[1])]
+    for copy in tables:
+        copy.start()
+    gather.relay()
+    gather.take((3, 7))
+    for copy in stores + [wo_store] + tables:
+        copy.wait()
+    gather.finish()
+
+
+def first_call(n, x_local, gain, wo_rows, freq):
+    n_batch, rows, width = x_local.shape
+    depth = wo_rows.shape[0]
+    seq = n * rows
+    hbm = pl.BlockSpec(memory_space=pl.ANY)
+    vmem = pl.BlockSpec(memory_space=pltpu.VMEM)
+    return pl.pallas_call(
+        functools.partial(first_kernel, n, n_batch),
+        in_specs=[hbm, vmem, hbm, vmem],
+        out_specs=[hbm] * (n_batch + 3),
+        out_shape=[jax.ShapeDtypeStruct((seq, width), jnp.bfloat16)] * n_batch
+        + [jax.ShapeDtypeStruct((n * depth, width), jnp.bfloat16)]
+        + [jax.ShapeDtypeStruct((seq, HEAD_DIM), jnp.float32)] * 2,
+        scratch_shapes=[
+            pltpu.VMEM((n_batch, rows, width), jnp.bfloat16),
+            pltpu.VMEM((n_batch, rows, width), jnp.bfloat16),
+            pltpu.VMEM((depth, width), jnp.bfloat16),
+            pltpu.VMEM((3, rows, width), jnp.bfloat16),
+            pltpu.VMEM((seq, HEAD_DIM), jnp.float32),
+            pltpu.VMEM((seq, HEAD_DIM), jnp.float32),
+            pltpu.SemaphoreType.DMA((n_batch,)),
+            pltpu.SemaphoreType.DMA((2,)),
+            pltpu.SemaphoreType.DMA((n_batch,)),
+            pltpu.SemaphoreType.DMA((2,)),
+        ] + GATHER_SEMS,
+        compiler_params=pltpu.CompilerParams(
+            collective_id=0, has_side_effects=True, vmem_limit_bytes=40 * 1024 * 1024),
+        cost_estimate=pl.CostEstimate(flops=100000000, bytes_accessed=seq * width * 4, transcendentals=seq * HEAD_DIM * 2),
+        name='first_gather',
+    )(x_local, gain, wo_rows, freq)
+
+
+def block_kernel(n, width, h_ref, wq_ref, wk_ref, wv_ref, qg_ref, kg_ref, cos_ref, sin_ref, next_in,
+                 o_hbm, next_buf, k_out, v_out,
+                 q_s, k_s, vt_s, stats, o_s, own_v, stage, own_sem, st_send, st_recv, o_send, o_recv, o_local, *gather_sems):
     step = pl.program_id(0)
     me = lax.axis_index('tp')
     tile = h_ref.shape[0]
@@ -49,28 +240,54 @@
                 src_ref=part, dst_ref=part, send_sem=st_send.at[d, chunk], recv_sem=st_recv.at[src, chunk],
                 device_id=peer(d), device_id_type=MESH).wait_recv()
 
+    gather = RingGather(next_buf, own_v, stage, me, *gather_sems)
+
+    def lay(x):
+        return x if len(k_out.shape) == 2 else x.reshape(x.shape[0], heads, HEAD_DIM)
+
     @pl.when(step == 0)
     def _():
-        barrier = pltpu.get_barrier_semaphore()
-        for d in range(1, n):
-            pl.semaphore_signal(barrier, inc=1, device_id=peer(d), device_id_type=MESH)
+        greet(n, me)
+        own_load = pltpu.make_async_copy(gather.block(me), own_v, own_sem)
+        own_load.start()
+        pl.semaphore_wait(pltpu.get_barrier_semaphore(), n - 1)
+        own_load.wait()
+        gather.send((0,))
+
+    @pl.when(step == 3)
+    def _():
+        gather.send((1,))
 
     @pl.when(step == half)
     def _():
-        pl.semaphore_wait(pltpu.get_barrier_semaphore(), n - 1)
         for d in range(1, n):
             stats_copy(0, d).start()
+
+    @pl.when(step == half + 2)
+    def _():
+        gather.send((2,))
+
+    @pl.when(step == n)
+    def _():
+        for d in range(1, n):
+            stats_copy(1, d).start()
+        gather.send((3,))
+
+    @pl.when(step == 3 * n)
+    def _():
+        gather.relay()
+
+    @pl.when(step == 3 * n + half)
+    def _():
+        gather.take((3, 7))
 
     @pl.when(step < n)
     def _():
         h = h_ref[...]
         q = jnp.dot(h, wq_ref[...], preferred_element_type=jnp.float32).astype(jnp.bfloat16)
         k = jnp.dot(h, wk_ref[...], preferred_element_type=jnp.float32).astype(jnp.bfloat16)
-        v = jnp.dot(h, wv_ref[...], preferred_element_type=jnp.float32).astype(jnp.bfloat16)
         q_s[step] = q
         k_s[step] = k
-        v_out[...] = v
-        vt_s[step] = v.T
         qf, kf = q.astype(jnp.float32), k.astype(jnp.float32)
         q_sq = jnp.sum(qf * qf, axis=1, keepdims=True)
         k_sq = jnp.sum(kf * kf, axis=1, keepdims=True)
@@ -82,19 +299,23 @@
             rows.append(both.T[:2])
         stats[me, step] = jnp.concatenate(rows, axis=0)
 
-    @pl.when(step == n)
-    def _():
-        for d in range(1, n):
-            stats_copy(1, d).start()
+    @pl.when((step >= n) & (step < 2 * n))
+    def _():
+        v = jnp.dot(h_ref[...], wv_ref[...], preferred_element_type=jnp.float32).astype(jnp.bfloat16)
+        v_out[...] = lay(v)
+        vt_s[step - n] = v.T
+
+    @pl.when(step == 2 * n)
+    def _():
         wait_stats(0)
 
-    @pl.when(step == n + half)
+    @pl.when(step == 2 * n + half)
     def _():
         wait_stats(1)
 
-    @pl.when((step >= n) & (step < 2 * n))
-    def _():
-        j = step - n
+    @pl.when((step >= 2 * n) & (step < 3 * n))
+    def _():
+        j = step - 2 * n
         total = stats[0, j]
         for s in range(1, n):
             total = total + stats[s, j]
@@ -112,7 +333,7 @@
                 rot = jnp.concatenate(outs, axis=1)
                 x_s[j, part, :] = rot
                 if x_s is k_s:
-                    k_out[part, :] = rot
+                    k_out[part] = lay(rot)
 
     def o_copy(d):
         return pltpu.make_async_remote_copy(
@@ -122,9 +343,9 @@
     def o_own():
         return pltpu.make_async_copy(o_s.at[0], o_hbm.at[:, pl.ds(pl.multiple_of(me * cols, cols), cols)], o_local)
 
-    @pl.when(step >= 2 * n)
-    def _():
-        d = lax.rem(step - 2 * n + 1, n)
+    @pl.when(step >= 3 * n)
+    def _():
+        d = lax.rem(step - 3 * n + 1, n)
         blk = lax.rem(me + d, n)
         scale = HEAD_DIM ** -0.5 * math.log2(math.e)
         nt = (((1,), (1,)), ((), ()))
@@ -176,8 +397,9 @@
         def _():
             o_own().start()
 
-    @pl.when(step == 3 * n - 1)
-    def _():
+    @pl.when(step == 4 * n - 1)
+    def _():
+        gather.finish()
         o_own().wait()
         for d in range(1, n):
             src = lax.rem(me + d, n)
@@ -189,89 +411,225 @@
                 stats_copy(chunk, d).wait_send()
 
 
-def block_call(n, h_full, wq, wk, wv, qg, kg, cos, sin):
+def block_call(n, h_full, wq, wk, wv, qg, kg, cos, sin, next_buf, cached):
     seq, width = h_full.shape
     cols = wq.shape[1]
     tile = seq // n
     heads = cols // HEAD_DIM
 
-    def first(i):
-        return (jnp.minimum(i, n - 1), 0)
+    def twice(i):
+        return (jnp.where(i < 2 * n, lax.rem(i, n), n - 1), 0)
 
     def second(i):
         return (jnp.clip(i - n, 0, n - 1), 0)
 
+    def third(i):
+        return (jnp.clip(i - 2 * n, 0, n - 1), 0)
+
     def whole(i):
         return (0, 0)
+
+    cache_tile = (tile, heads, HEAD_DIM) if cached else (tile, cols)
+    cache_shape = (seq,) + cache_tile[1:]
+    hbm = pl.BlockSpec(memory_space=pl.ANY)
+
+    def cache_map(index):
+        return (lambda i: index(i) + (0,)) if cached else index
 
     flops = 2 * seq * width * cols * 3 + 2 * seq * seq * cols * 2
     return pl.pallas_call(
         functools.partial(block_kernel, n, width),
-        grid=(3 * n,),
+        grid=(4 * n,),
         in_specs=[
-            pl.BlockSpec((tile, width), first),
+            pl.BlockSpec((tile, width), twice),
             pl.BlockSpec((width, cols), whole), pl.BlockSpec((width, cols), whole), pl.BlockSpec((width, cols), whole),
             pl.BlockSpec((1, cols), whole), pl.BlockSpec((1, cols), whole),
-            pl.BlockSpec((tile, HEAD_DIM), second), pl.BlockSpec((tile, HEAD_DIM), second),
+            pl.BlockSpec((tile, HEAD_DIM), third), pl.BlockSpec((tile, HEAD_DIM), third),
+            hbm,
         ],
         out_specs=[
-            pl.BlockSpec(memory_space=pl.ANY),
-            pl.BlockSpec((tile, cols), second),
-            pl.BlockSpec((tile, cols), first),
+            hbm, hbm,
+            pl.BlockSpec(cache_tile, cache_map(third)),
+            pl.BlockSpec(cache_tile, cache_map(second)),
         ],
         out_shape=[
             jax.ShapeDtypeStruct((tile, n * cols), jnp.bfloat16),
-            jax.ShapeDtypeStruct((seq, cols), jnp.bfloat16),
-            jax.ShapeDtypeStruct((seq, cols), jnp.bfloat16),
+            jax.ShapeDtypeStruct(next_buf.shape, next_buf.dtype),
+            jax.ShapeDtypeStruct(cache_shape, jnp.bfloat16),
+            jax.ShapeDtypeStruct(cache_shape, jnp.bfloat16),
         ],
+        input_output_aliases={8: 1},
         scratch_shapes=[
             pltpu.VMEM((n, tile, cols), jnp.bfloat16),
             pltpu.VMEM((n, tile, cols), jnp.bfloat16),
             pltpu.VMEM((n, cols, tile), jnp.bfloat16),
             pltpu.VMEM((n, n, 2 * tile // HEAD_DIM, HEAD_DIM), jnp.float32),
             pltpu.VMEM((n, tile, cols), jnp.bfloat16),
+            pltpu.VMEM((next_buf.shape[0] // n, width), jnp.bfloat16),
+            pltpu.VMEM((3, next_buf.shape[0] // n, width), jnp.bfloat16),
+            pltpu.SemaphoreType.DMA,
             pltpu.SemaphoreType.DMA((n, 2)),
             pltpu.SemaphoreType.DMA((n, 2)),
             pltpu.SemaphoreType.DMA((n,)),
             pltpu.SemaphoreType.DMA((n,)),
             pltpu.SemaphoreType.DMA,
+        ] + GATHER_SEMS,
+        compiler_params=pltpu.CompilerParams(
+            collective_id=1 if cached else 2, has_side_effects=True, vmem_limit_bytes=52 * 1024 * 1024,
+            dimension_semantics=('arbitrary',)),
+        cost_estimate=pl.CostEstimate(flops=flops, bytes_accessed=seq * width * 2 + 6 * seq * cols * 2, transcendentals=seq * seq * heads // 2),
+        name='attn_block' if cached else 'attn_last',
+    )(h_full, wq, wk, wv, qg, kg, cos, sin, next_buf)
+
+
+N_CHUNK = 4
+
+
+def last_kernel(n_batch, *refs):
+    x_ref, wo_hbm = refs[:2]
+    o_hbm = refs[2:2 + n_batch]
+    rest = refs[2 + n_batch:]
+    caches = rest[:2 * (n_batch - 1)]
+    k_last, v_last = rest[2 * (n_batch - 1):2 * n_batch]
+    out_ref, k_cache, v_cache = rest[2 * n_batch:2 * n_batch + 3]
+    w_v, o_v, c_v, l_v, w_sem, o_sem, ci_sem, co_sem, lo_sem = rest[2 * n_batch + 3:]
+    step = pl.program_id(0)
+    b, j = step // N_CHUNK, lax.rem(step, N_CHUNK)
+    chunk = w_v.shape[2]
+    rows = c_v.shape[1]
+    per = caches[0].shape[0] // rows
+    slots = c_v.shape[0]
+
+    def w_copy(c):
+        return pltpu.make_async_copy(wo_hbm.at[:, pl.ds(c * chunk, chunk)], w_v.at[c], w_sem.at[c])
+
+    def o_copy(i):
+        return pltpu.make_async_copy(o_hbm[i], o_v.at[i], o_sem.at[i])
+
+    @pl.when(step == 0)
+    def _():
+        w_copy(0).start()
+        o_copy(0).start()
+        for c in range(1, N_CHUNK):
+            w_copy(c).start()
+        for i in range(1, n_batch):
+            o_copy(i).start()
+
+    for i in range(n_batch):
+        @pl.when(step == i * N_CHUNK)
+        def _(i=i):
+            o_copy(i).wait()
+    for c in range(N_CHUNK):
+        @pl.when(step == c)
+        def _(c=c):
+            w_copy(c).wait()
+
+    items = [(i, part) for i in range(len(caches)) for part in range(per)]
+
+    def item_in(t):
+        i, part = items[t]
+        return pltpu.make_async_copy(caches[i].at[pl.ds(part * rows, rows)], c_v.at[t % slots], ci_sem.at[t % slots])
+
+    def item_out(t):
+        i, part = items[t]
+        cache = k_cache if i % 2 == 0 else v_cache
+        return pltpu.make_async_copy(c_v.at[t % slots], cache.at[i // 2, pl.ds(part * rows, rows)], co_sem.at[t % slots])
+
+    for t in range(len(items) + slots):
+        @pl.when(step == t)
+        def _(t=t):
+            if t >= slots:
+                item_out(t - slots).wait()
+            if t < len(items):
+                item_in(t).start()
+            if 1 <= t <= len(items):
+                item_in(t - 1).wait()
+                item_out(t - 1).start()
+
+    last_rows = l_v.shape[2]
+
+    def last_out(which, t):
+        cache = (k_cache, v_cache)[which]
+        return pltpu.make_async_copy(l_v.at[which, lax.rem(t, 2)],
+                                     cache.at[n_batch - 1, pl.ds(pl.multiple_of(t * last_rows, last_rows), last_rows)],
+                                     lo_sem.at[which, lax.rem(t, 2)])
+
+    @pl.when(step >= 2)
+    def _():
+        for which in range(2):
+            last_out(which, step - 2).wait()
+    for which, src in enumerate((k_last, v_last)):
+        l_v[which, lax.rem(step, 2)] = src[...].reshape(l_v.shape[2:])
+        last_out(which, step).start()
+
+    y = jnp.dot(o_v[b], w_v[j], preferred_element_type=jnp.float32).astype(jnp.bfloat16)
+    out_ref[0] = (x_ref[0].astype(jnp.float32) + y.astype(jnp.float32)).astype(jnp.bfloat16)
+
+    @pl.when(step == n_batch * N_CHUNK - 1)
+    def _():
+        for which in range(2):
+            for back in (1, 0):
+                last_out(which, step - back).wait()
+
+
+def last_call(x_local, w_o, os, ks, vs):
+    n_batch, rows, width = x_local.shape
+    seq, heads, _ = ks[0].shape
+    steps = n_batch * N_CHUNK
+    hbm = pl.BlockSpec(memory_space=pl.ANY)
+    block = pl.BlockSpec((1, rows, width // N_CHUNK), lambda i: (i // N_CHUNK, 0, lax.rem(i, N_CHUNK)))
+    last = pl.BlockSpec((seq // steps, heads * HEAD_DIM), lambda i: (i, 0))
+    caches = [c for pair in zip(ks[:-1], vs[:-1]) for c in pair]
+    cache = jax.ShapeDtypeStruct((n_batch, seq, heads, HEAD_DIM), jnp.bfloat16)
+    return pl.pallas_call(
+        functools.partial(last_kernel, n_batch),
+        grid=(steps,),
+        in_specs=[block, hbm] + [hbm] * (n_batch + len(caches)) + [last, last],
+        out_specs=[block, hbm, hbm],
+        out_shape=[jax.ShapeDtypeStruct(x_local.shape, jnp.bfloat16), cache, cache],
+        scratch_shapes=[
+            pltpu.VMEM((N_CHUNK, w_o.shape[0], width // N_CHUNK), jnp.bfloat16),
+            pltpu.VMEM((n_batch, rows, w_o.shape[0]), jnp.bfloat16),
+            pltpu.VMEM((4, 2048, heads, HEAD_DIM), jnp.bfloat16),
+            pltpu.VMEM((2, 2, seq // steps, heads, HEAD_DIM), jnp.bfloat16),
+            pltpu.SemaphoreType.DMA((N_CHUNK,)),
+            pltpu.SemaphoreType.DMA((n_batch,)),
+            pltpu.SemaphoreType.DMA((4,)),
+            pltpu.SemaphoreType.DMA((4,)),
+            pltpu.SemaphoreType.DMA((2, 2)),
         ],
         compiler_params=pltpu.CompilerParams(
-            collective_id=0, has_side_effects=True, vmem_limit_bytes=52 * 1024 * 1024,
-            dimension_semantics=('arbitrary',)),
-        cost_estimate=pl.CostEstimate(flops=flops, bytes_accessed=seq * width * 2 + 6 * seq * cols * 2, transcendentals=seq * seq * heads // 2),
-        name='attn_block',
-    )(h_full, wq, wk, wv, qg, kg, cos, sin)
+            vmem_limit_bytes=52 * 1024 * 1024, dimension_semantics=('arbitrary',)),
+        cost_estimate=pl.CostEstimate(flops=2 * n_batch * rows * width * w_o.shape[0],
+                                      bytes_accessed=8 * n_batch * rows * width * 2, transcendentals=0),
+        name='last_proj',
+    )(x_local, w_o, *os, *caches, ks[-1], vs[-1])
 
 
 def solution(mesh):
     n = mesh.shape['tp']
+    assert n == 8 and tuple(mesh.axis_names) == ('dp', 'tp')
 
     def local_block(x_local, attn_gain, wq, wk, wv, qg, kg, wo_rows):
         n_batch, rows, width = x_local.shape
-        seq = rows * n
         cols = wq.shape[1]
-        cos, sin = rope_tables(seq)
         qg2, kg2 = qg.reshape(1, cols), kg.reshape(1, cols)
-        gathered = []
-        for b in range(n_batch):
-            x_f32 = x_local[b].astype(jnp.float32)
-            inv_rms = lax.rsqrt(jnp.mean(x_f32 * x_f32, axis=-1, keepdims=True) + EPS)
-            normed = (x_f32 * inv_rms * attn_gain).astype(jnp.bfloat16)
-            gathered.append(lax.all_gather(normed, 'tp', axis=0, tiled=True))
-        wo_src, gathered[-1] = lax.optimization_barrier((wo_rows, gathered[-1]))
-        w_o = lax.all_gather(wo_src, 'tp', axis=0, tiled=True)
+        half_dim = HEAD_DIM // 2
+        inv_freq = 10000.0 ** (-jnp.arange(half_dim, dtype=jnp.float32) * (2.0 / HEAD_DIM))
+        freq = jnp.concatenate([inv_freq, inv_freq]).reshape(1, HEAD_DIM)
+        *hs, w_o, cos, sin = first_call(n, x_local, attn_gain.reshape(1, width), wo_rows, freq)
         os, ks, vs = [], [], []
         for b in range(n_batch):
-            o, k, v = block_call(n, gathered[b], wq, wk, wv, qg2, kg2, cos, sin)
+            more = b + 1 < n_batch
+            o, gathered, k, v = block_call(n, hs[b], wq, wk, wv, qg2, kg2, cos, sin, hs[b + 1] if more else w_o, more)
+            if more:
+                hs[b + 1] = gathered
+            else:
+                w_o = gathered
             os.append(o)
             ks.append(k)
             vs.append(v)
-        o_all = jnp.stack(os)
-        y = jnp.einsum('btc,cd->btd', o_all, w_o, preferred_element_type=jnp.float32).astype(jnp.bfloat16)
-        hidden_out = (x_local.astype(jnp.float32) + y.astype(jnp.float32)).astype(jnp.bfloat16)
-        cache_shape = (n_batch, seq, cols // HEAD_DIM, HEAD_DIM)
-        return hidden_out, jnp.stack(ks).reshape(cache_shape), jnp.stack(vs).reshape(cache_shape)
+        return tuple(last_call(x_local, w_o, os, ks, vs))
 
     seq_spec = P('dp', 'tp', None)
     head_spec = P('dp', None, 'tp', None)

time: 597 us -> 510 us (0.85)
  Pallas kernels: 345 us -> 499 us
  waiting for transfers between devices: 125 us -> 0 us
  other arithmetic: 54.1 us -> 0.09 us
  matrix products: 25 us -> 0 us
  local copies, waits for them, and re-layouts: 31.7 us -> 7.77 us
  between operations: 13.9 us -> 0.85 us
    pallas_call x4 -> x6, Pallas kernels: 345 us -> 499 us  [the longest x4 388 us: block_call(): pl.pallas_call(functools.partial(block_kernel, n, width), grid=(4 * n,),...]
    all_gather x5 -> x0, waiting for transfers between devices: 123 us -> none  [the longest x4 123 us: local_block(): gathered.append(lax.all_gather(normed, 'tp', axis=0, tiled=True))]
    another operation x2 -> x0, other arithmetic: 34.4 us -> none  [the longest x1 17.9 us: local_block(): jnp.stack(ks).reshape(cache_shape)]
    another operation x8 -> x0, local copies, waits for them, and re-layouts: 30.3 us -> none  [the longest x4 15.9 us: local_block(): jnp.stack(ks).reshape(cache_shape)]
    dot_general x1 -> x0, matrix products: 25 us -> none  [local_block(): jnp.einsum('btc,cd->btd', o_all, w_o, preferred_element_type=jnp.float32)]
    neg x1 -> x0, other arithmetic: 7.83 us -> none  [rope_tables(): -sin]
    unnamed x16, local copies, waits for them, and re-layouts: 1.4 us -> 7.77 us
  transfers between devices with their start and end apart: 5 -> 0, of which waited for: 4 -> 0; matrix products, arithmetic and copies ran while one was open for 13% -> 0% of each run, Pallas kernels for 58% -> 0%
where the time goes in v2:
time: 510 us; the launch traced here: 507 us
  Pallas kernels  499 us (98%)
  local copies, waits for them, and re-layouts  7.77 us (2%)
    pallas_call x4, Pallas kernels, block_call(): pl.pallas_call(functools.partial(block_kernel, n, width), grid=(4 * n,),...  388 us
    pallas_call x1, Pallas kernels, first_call(): pl.pallas_call(functools.partial(first_kernel, n, n_batch), in_specs=[hbm...  76.6 us
    pallas_call x1, Pallas kernels, last_call(): pl.pallas_call(functools.partial(last_kernel, n_batch), grid=(steps,), in...  34 us

profile of v2, /device:TPU:7, one launch (start us, length us, event | category | flops | bytes accessed | tf_op | source)
XLA Modules:
  0.0 507.4 jit_solution(4339728142414275960)
XLA Ops:
  0.6 0.1 maximum_bitcast_fusion.freq_ref
  0.7 0.0 copy-start
  0.7 1.2 copy-done
  1.9 0.0 copy-start.1
  2.0 0.7 copy-done.1
  2.6 0.0 copy-start.5
  2.6 0.0 copy-start.6
  2.7 0.0 copy-start.7
  2.7 76.6 %first_gather.1 = (bf16[4096,2048]{1,0:T(8,128)(2,1)}, bf16[4096,2048]{1,0:T(8,128)(2,1)}, bf16[4096,2048]{1,0:T(8,128)(2,1)}, bf16[4096,2048]{1,0:T(8,128)(2,1)...) custom-call(bf16[4,512,2048]{2,1,0:T(8,128)(2,1)} %refs_0_.1, ...), custom_call_target="tpu_custom_call" | custom-call | flops 100000000 | bytes 33554432 | tf_op jit(solution)/shard_map/first_gather/pallas_call | solution.py:189
  79.2 0.0 copy-start.2
  79.2 3.2 copy-done.2
  82.4 0.0 copy-start.3
  82.4 1.3 copy-done.3
  83.7 0.0 copy-start.4
  83.7 1.3 copy-done.4
  85.1 0.0 copy-done.5
  85.1 0.0 copy-done.6
  85.1 0.0 copy-done.7
  85.1 100.9 %attn_block.3 = (bf16[512,2048]{1,0:T(8,128)(2,1)}, bf16[4096,2048]{1,0:T(8,128)(2,1)}, bf16[4096,2,128]{2,1,0:T(2,128)(2,1)}, bf16[4096,2,128]{2,1,0:T(2,128)(2,1)}) custom-call(bf16[4096,2048]{1,0:T(8,128)(2,1)} %get-tuple-element.26.h_ref, bf16[2048,256]{1,0:T(8,128)(2,1)S(1)} %copy-done.5, ...), custom_call_target="tpu_custom_call", output_to_operand_aliasing={{1}: (8, {})} | custom-call | flops 30064771072 | bytes 29360128 | tf_op jit(solution)/shard_map/attn_block/pallas_call | solution.py:440
  186.0 100.8 %attn_block.4 = (bf16[512,2048]{1,0:T(8,128)(2,1)}, bf16[4096,2048]{1,0:T(8,128)(2,1)}, bf16[4096,2,128]{2,1,0:T(2,128)(2,1)}, bf16[4096,2,128]{2,1,0:T(2,128)(2,1)}) custom-call(bf16[4096,2048]{1,0:T(8,128)(2,1)} %get-tuple-element.30.h_ref, bf16[2048,256]{1,0:T(8,128)(2,1)S(1)} %copy-done.5, ...), custom_call_target="tpu_custom_call", output_to_operand_aliasing={{1}: (8, {})} | custom-call | flops 30064771072 | bytes 29360128 | tf_op jit(solution)/shard_map/attn_block/pallas_call | solution.py:440
  286.8 100.5 %attn_block.5 = (bf16[512,2048]{1,0:T(8,128)(2,1)}, bf16[4096,2048]{1,0:T(8,128)(2,1)}, bf16[4096,2,128]{2,1,0:T(2,128)(2,1)}, bf16[4096,2,128]{2,1,0:T(2,128)(2,1)}) custom-call(bf16[4096,2048]{1,0:T(8,128)(2,1)} %get-tuple-element.32.h_ref, bf16[2048,256]{1,0:T(8,128)(2,1)S(1)} %copy-done.5, ...), custom_call_target="tpu_custom_call", output_to_operand_aliasing={{1}: (8, {})} | custom-call | flops 30064771072 | bytes 29360128 | tf_op jit(solution)/shard_map/attn_block/pallas_call | solution.py:440
  387.3 86.0 %attn_last.1 = (bf16[512,2048]{1,0:T(8,128)(2,1)}, bf16[2048,2048]{1,0:T(8,128)(2,1)}, bf16[4096,256]{1,0:T(8,128)(2,1)}, bf16[4096,256]{1,0:T(8,128)(2,1)}) custom-call(bf16[4096,2048]{1,0:T(8,128)(2,1)} %get-tuple-element.34.h_ref, bf16[2048,256]{1,0:T(8,128)(2,1)S(1)} %copy-done.5, bf16[2048,256]{1,0:T(8,128)(2,1)} %wk_ref.7, ...), custom_call_target="tpu_custom_call", output_to_operand_aliasing={{1}: (8, {})} | custom-call | flops 30064771072 | bytes 29360128 | tf_op jit(solution)/shard_map/attn_last/pallas_call | solution.py:440
  473.3 34.0 %last_proj.1 = (bf16[4,512,2048]{2,1,0:T(8,128)(2,1)}, bf16[4,4096,2,128]{3,2,1,0:T(2,128)(2,1)}, bf16[4,4096,2,128]{3,2,1,0:T(2,128)(2,1)}) custom-call(bf16[4,512,2048]{2,1,0:T(8,128)(2,1)} %refs_0_.1, bf16[2048,2048]{1,0:T(8,128)(2,1)} %get-tuple-element.36.refs_1_, bf16[512,2048]{1,0:T(8,128)(2,1)} %get-tuple-element.37.refs_2_, ...), custom_call_target="tpu_custom_call" | custom-call | flops 17179869184 | bytes 67108864 | tf_op jit(solution)/shard_map/last_proj/pallas_call | solution.py:584
  (1 shorter events, 0.0 us)
Async XLA Ops:
  0.7 1.2 copy-start
  1.9 0.7 copy-start.1
  2.6 82.4 %copy-start.5 = (bf16[2048,256]{1,0:T(8,128)(2,1)S(1)}, bf16[2048,256]{1,0:T(8,128)(2,1)}, u32[]{:S(2)}) copy-start(bf16[2048,256]{1,0:T(8,128)(2,1)} %wq_ref.7) | copy-start | bytes 3145732
  2.6 82.4 %copy-start.6 = (f32[256]{0:T(256)S(1)}, f32[256]{0:T(256)}, u32[]{:S(2)}) copy-start(f32[256]{0:T(256)} %param.13) | copy-start | bytes 3076
  2.7 82.4 %copy-start.7 = (f32[256]{0:T(256)S(1)}, f32[256]{0:T(256)}, u32[]{:S(2)}) copy-start(f32[256]{0:T(256)} %param.14) | copy-start | bytes 3076
  79.2 3.2 copy-start.2
  82.4 1.3 copy-start.3
  83.7 1.3 copy-start.4

commit v3 on v2

--- a/solution.py
+++ b/solution.py
@@ -133,23 +133,28 @@
               for b in range(n_batch)]
     loads[0].start()
 
-    def norm(b):
+    def norm(b, first=0, strips=rows // 64):
         def body(r, carry):
             part = pl.ds(pl.multiple_of(r * 64, 64), 64)
             x = x_v[b, part, :].astype(jnp.float32)
             inv = lax.rsqrt(jnp.mean(x * x, axis=-1, keepdims=True) + EPS)
             h_v[b, part, :] = (x * inv * gain_ref[...]).astype(jnp.bfloat16)
             return carry
-        lax.fori_loop(0, rows // 64, body, 0)
+        lax.fori_loop(first, first + strips, body, 0)
 
     loads[0].wait()
     for load in loads[1:]:
         load.start()
     wo_load.start()
-    norm(0)
+    quarter = rows // 256
+    norm(0, 0, quarter)
+    norm(0, 2 * quarter, quarter)
     pl.semaphore_wait(pltpu.get_barrier_semaphore(), n - 1)
     gather = RingGather(h0, h_v.at[0], stage, me, *gather_sems)
-    gather.send((0, 1, 2, 3))
+    gather.send((0,))
+    norm(0, quarter, quarter)
+    norm(0, 3 * quarter, quarter)
+    gather.send((1, 2, 3))
     stores[0].start()
     for b in range(1, n_batch):
         loads[b].wait()
@@ -206,22 +211,27 @@
             pltpu.SemaphoreType.DMA((2,)),
         ] + GATHER_SEMS,
         compiler_params=pltpu.CompilerParams(
-            collective_id=0, has_side_effects=True, vmem_limit_bytes=40 * 1024 * 1024),
+            collective_id=0, has_side_effects=True, vmem_limit_bytes=62 * 1024 * 1024),
         cost_estimate=pl.CostEstimate(flops=100000000, bytes_accessed=seq * width * 4, transcendentals=seq * HEAD_DIM * 2),
         name='first_gather',
     )(x_local, gain, wo_rows, freq)
 
 
-def block_kernel(n, width, h_ref, wq_ref, wk_ref, wv_ref, qg_ref, kg_ref, cos_ref, sin_ref, next_in,
+AHEAD = 2
+
+
+def block_kernel(n, width, h_hbm, wq_hbm, wk_hbm, wv_hbm, qg_ref, kg_ref, cos_hbm, sin_hbm, next_in,
                  o_hbm, next_buf, k_out, v_out,
-                 q_s, k_s, vt_s, stats, o_s, own_v, stage, own_sem, st_send, st_recv, o_send, o_recv, o_local, *gather_sems):
-    step = pl.program_id(0)
+                 h_v, wqk_v, wv_v, cos_v, sin_v, q_s, k_s, vt_s, k_st, v_st, stats, o_s, s_buf, p_buf, acc_buf, own_v, stage,
+                 h_sem, w_sem, tab_sem, kv_sem, own_sem, st_send, st_recv, o_send, o_recv, o_local, *gather_sems):
     me = lax.axis_index('tp')
-    tile = h_ref.shape[0]
-    cols = wq_ref.shape[1]
+    tile = h_v.shape[1]
+    cols = wv_v.shape[1]
     heads = cols // HEAD_DIM
     groups = tile // HEAD_DIM
     half = n // 2
+    gather = RingGather(next_buf, own_v, stage, me, *gather_sems)
+    scale = HEAD_DIM ** -0.5 * math.log2(math.e)
 
     def peer(d):
         return {'tp': lax.rem(me + d, n)}
@@ -231,6 +241,10 @@
         return pltpu.make_async_remote_copy(
             src_ref=part, dst_ref=part, send_sem=st_send.at[d, chunk], recv_sem=st_recv.at[me, chunk],
             device_id=peer(d), device_id_type=MESH)
+
+    def send_stats(chunk):
+        for d in range(1, n):
+            stats_copy(chunk, d).start()
 
     def wait_stats(chunk):
         for d in range(1, n):
@@ -240,54 +254,49 @@
                 src_ref=part, dst_ref=part, send_sem=st_send.at[d, chunk], recv_sem=st_recv.at[src, chunk],
                 device_id=peer(d), device_id_type=MESH).wait_recv()
 
-    gather = RingGather(next_buf, own_v, stage, me, *gather_sems)
-
     def lay(x):
         return x if len(k_out.shape) == 2 else x.reshape(x.shape[0], heads, HEAD_DIM)
 
-    @pl.when(step == 0)
-    def _():
-        greet(n, me)
-        own_load = pltpu.make_async_copy(gather.block(me), own_v, own_sem)
-        own_load.start()
-        pl.semaphore_wait(pltpu.get_barrier_semaphore(), n - 1)
-        own_load.wait()
-        gather.send((0,))
-
-    @pl.when(step == 3)
-    def _():
-        gather.send((1,))
-
-    @pl.when(step == half)
-    def _():
-        for d in range(1, n):
-            stats_copy(0, d).start()
-
-    @pl.when(step == half + 2)
-    def _():
-        gather.send((2,))
-
-    @pl.when(step == n)
-    def _():
-        for d in range(1, n):
-            stats_copy(1, d).start()
-        gather.send((3,))
-
-    @pl.when(step == 3 * n)
-    def _():
-        gather.relay()
-
-    @pl.when(step == 3 * n + half)
-    def _():
-        gather.take((3, 7))
-
-    @pl.when(step < n)
-    def _():
-        h = h_ref[...]
-        q = jnp.dot(h, wq_ref[...], preferred_element_type=jnp.float32).astype(jnp.bfloat16)
-        k = jnp.dot(h, wk_ref[...], preferred_element_type=jnp.float32).astype(jnp.bfloat16)
-        q_s[step] = q
-        k_s[step] = k
+    def hcols(hd):
+        return slice(hd * HEAD_DIM, (hd + 1) * HEAD_DIM)
+
+    def rows_of(i):
+        return pl.ds(pl.multiple_of(i * tile, tile), tile)
+
+    def h_load(i):
+        return pltpu.make_async_copy(h_hbm.at[rows_of(i)], h_v.at[i], h_sem.at[i])
+
+    def kv_store(which, i):
+        src, dst = ((k_st, k_out), (v_st, v_out))[which]
+        return pltpu.make_async_copy(src.at[i], dst.at[rows_of(i)], kv_sem.at[which, i])
+
+    w_loads = [
+        pltpu.make_async_copy(wq_hbm, wqk_v.at[:, pl.ds(0, cols)], w_sem.at[0]),
+        pltpu.make_async_copy(wk_hbm, wqk_v.at[:, pl.ds(cols, cols)], w_sem.at[1]),
+        pltpu.make_async_copy(wv_hbm, wv_v, w_sem.at[2])]
+    tab_loads = [pltpu.make_async_copy(cos_hbm, cos_v, tab_sem.at[0]), pltpu.make_async_copy(sin_hbm, sin_v, tab_sem.at[1])]
+    own_load = pltpu.make_async_copy(gather.block(me), own_v, own_sem)
+
+    greet(n, me)
+    own_load.start()
+    for load in w_loads[:2] + [h_load(i) for i in range(AHEAD)] + w_loads[2:]:
+        load.start()
+    own_load.wait()
+    pl.semaphore_wait(pltpu.get_barrier_semaphore(), n - 1)
+    gather.send((0,))
+    for load in w_loads[:2]:
+        load.wait()
+
+    def qk_block(i, carry):
+        @pl.when(i + AHEAD < n)
+        def _():
+            h_load(i + AHEAD).start()
+
+        h_load(i).wait()
+        qk = jnp.dot(h_v[i], wqk_v[...], preferred_element_type=jnp.float32).astype(jnp.bfloat16)
+        q, k = qk[:, :cols], qk[:, cols:]
+        q_s[i] = q
+        k_s[i] = k
         qf, kf = q.astype(jnp.float32), k.astype(jnp.float32)
         q_sq = jnp.sum(qf * qf, axis=1, keepdims=True)
         k_sq = jnp.sum(kf * kf, axis=1, keepdims=True)
@@ -297,43 +306,57 @@
             part = slice(g * HEAD_DIM, (g + 1) * HEAD_DIM)
             both = jnp.where(lane == 0, q_sq[part], k_sq[part])
             rows.append(both.T[:2])
-        stats[me, step] = jnp.concatenate(rows, axis=0)
-
-    @pl.when((step >= n) & (step < 2 * n))
-    def _():
-        v = jnp.dot(h_ref[...], wv_ref[...], preferred_element_type=jnp.float32).astype(jnp.bfloat16)
-        v_out[...] = lay(v)
-        vt_s[step - n] = v.T
-
-    @pl.when(step == 2 * n)
-    def _():
-        wait_stats(0)
-
-    @pl.when(step == 2 * n + half)
-    def _():
-        wait_stats(1)
-
-    @pl.when((step >= 2 * n) & (step < 3 * n))
-    def _():
-        j = step - 2 * n
+        stats[me, i] = jnp.concatenate(rows, axis=0)
+        return carry
+
+    lax.fori_loop(0, half, qk_block, 0)
+    for load in tab_loads:
+        load.start()
+    send_stats(0)
+    gather.send((1,))
+    lax.fori_loop(half, n, qk_block, 0)
+    send_stats(1)
+    gather.send((2, 3))
+    w_loads[2].wait()
+
+    def v_block(i, carry):
+        v = jnp.dot(h_v[i], wv_v[...], preferred_element_type=jnp.float32).astype(jnp.bfloat16)
+        v_st[i] = lay(v)
+        kv_store(1, i).start()
+        vt_s[i] = v.T
+        return carry
+
+    lax.fori_loop(0, n, v_block, 0)
+    for load in tab_loads:
+        load.wait()
+
+    def norm_block(j, carry):
         total = stats[0, j]
-        for s in range(1, n):
-            total = total + stats[s, j]
+        for src in range(1, n):
+            total = total + stats[src, j]
         inv = lax.rsqrt(total / width + EPS)
         inv_cols = jnp.concatenate([inv] * (HEAD_DIM // inv.shape[0]), axis=0).T
         for g in range(groups):
             part = slice(g * HEAD_DIM, (g + 1) * HEAD_DIM)
-            cos, sin = cos_ref[part, :], sin_ref[part, :]
+            tab = pl.ds(pl.multiple_of(j * tile + g * HEAD_DIM, HEAD_DIM), HEAD_DIM)
+            cos, sin = cos_v[tab, :], sin_v[tab, :]
             for x_s, g_ref, col in ((q_s, qg_ref, 2 * g), (k_s, kg_ref, 2 * g + 1)):
                 x = x_s[j, part, :].astype(jnp.float32) * inv_cols[:, col:col + 1] * g_ref[...]
                 outs = []
                 for hd in range(heads):
-                    xh = x[:, hd * HEAD_DIM:(hd + 1) * HEAD_DIM]
+                    xh = x[:, hcols(hd)]
                     outs.append((xh * cos + pltpu.roll(xh, HEAD_DIM // 2, 1) * sin).astype(jnp.bfloat16))
                 rot = jnp.concatenate(outs, axis=1)
                 x_s[j, part, :] = rot
                 if x_s is k_s:
-                    k_out[part] = lay(rot)
+                    k_st[j, part] = lay(rot)
+        kv_store(0, j).start()
+        return carry
+
+    wait_stats(0)
+    lax.fori_loop(0, half, norm_block, 0)
+    wait_stats(1)
+    lax.fori_loop(half, n, norm_block, 0)
 
     def o_copy(d):
         return pltpu.make_async_remote_copy(
@@ -343,51 +366,54 @@
     def o_own():
         return pltpu.make_async_copy(o_s.at[0], o_hbm.at[:, pl.ds(pl.multiple_of(me * cols, cols), cols)], o_local)
 
-    @pl.when(step >= 3 * n)
-    def _():
-        d = lax.rem(step - 3 * n + 1, n)
+    nt = (((1,), (1,)), ((), ()))
+    strip = 64
+
+    def softmax_step(j, hd, m, l):
+        top = None
+        for c in range(tile // strip):
+            part = jnp.max(s_buf[hd, c * strip:(c + 1) * strip, :].reshape(strip // 8, 8, tile), axis=0)
+            top = part if top is None else jnp.maximum(top, part)
+        m_new = jnp.max(top, axis=0, keepdims=True)
+        if m is not None:
+            m_new = jnp.maximum(m, m_new)
+        m_scaled = m_new * scale
+        total = None
+        for c in range(tile // strip):
+            p = jnp.exp2(s_buf[hd, c * strip:(c + 1) * strip, :] * scale - m_scaled)
+            part = jnp.sum(p.reshape(strip // 8, 8, tile), axis=0)
+            total = part if total is None else total + part
+            p_buf[hd, c * strip:(c + 1) * strip, :] = p.astype(jnp.bfloat16)
+        l_new = jnp.sum(total, axis=0, keepdims=True)
+        pv = jnp.dot(vt_s[j, hcols(hd), :], p_buf[hd], preferred_element_type=jnp.float32)
+        if m is None:
+            acc_buf[hd] = pv
+        else:
+            alpha = jnp.exp2((m - m_new) * scale)
+            l_new = l * alpha + l_new
+            acc_buf[hd] = acc_buf[hd] * alpha + pv
+        return m_new, l_new
+
+    def attend(step, carry):
+        d = lax.rem(step + 1, n)
         blk = lax.rem(me + d, n)
-        scale = HEAD_DIM ** -0.5 * math.log2(math.e)
-        nt = (((1,), (1,)), ((), ()))
-
-        def hcols(hd):
-            return slice(hd * HEAD_DIM, (hd + 1) * HEAD_DIM)
-
-        qs = [q_s[blk, :, hcols(hd)] for hd in range(heads)]
 
         def scores(j, hd):
-            return lax.dot_general(k_s[j, :, hcols(hd)], qs[hd], nt, preferred_element_type=jnp.float32)
-
-        key_pos = lax.broadcasted_iota(jnp.int32, (tile, tile), 0)
-        query_pos = lax.broadcasted_iota(jnp.int32, (tile, tile), 1)
-        keep = key_pos <= query_pos
-        carry = []
+            return lax.dot_general(k_s[j, :, hcols(hd)], q_s[blk, :, hcols(hd)], nt, preferred_element_type=jnp.float32)
+
+        keep = lax.broadcasted_iota(jnp.int32, (tile, tile), 0) <= lax.broadcasted_iota(jnp.int32, (tile, tile), 1)
         for hd in range(heads):
-            s = jnp.where(keep, scores(blk, hd), -jnp.inf)
-            m = jnp.max(s, axis=0, keepdims=True)
-            p = jnp.exp2(s * scale - m * scale)
-            l = jnp.sum(p, axis=0, keepdims=True)
-            acc = jnp.dot(vt_s[blk, hcols(hd), :], p.astype(jnp.bfloat16), preferred_element_type=jnp.float32)
-            carry.append((m, l, acc))
-
-        def body(j, carry):
-            out = []
-            ss = [scores(j, hd) for hd in range(heads)]
+            s_buf[hd] = jnp.where(keep, scores(blk, hd), -jnp.inf)
+        state = tuple(softmax_step(blk, hd, None, None) for hd in range(heads))
+
+        def body(j, state):
             for hd in range(heads):
-                m, l, acc = carry[hd]
-                s = ss[hd]
-                m_new = jnp.maximum(m, jnp.max(s, axis=0, keepdims=True))
-                alpha = jnp.exp2((m - m_new) * scale)
-                p = jnp.exp2(s * scale - m_new * scale)
-                l = l * alpha + jnp.sum(p, axis=0, keepdims=True)
-                acc = acc * alpha + jnp.dot(vt_s[j, hcols(hd), :], p.astype(jnp.bfloat16), preferred_element_type=jnp.float32)
-                out.append((m_new, l, acc))
-            return tuple(out)
-
-        carry = lax.fori_loop(0, blk, body, tuple(carry))
+                s_buf[hd] = scores(j, hd)
+            return tuple(softmax_step(j, hd, *state[hd]) for hd in range(heads))
+
+        state = lax.fori_loop(0, blk, body, state)
         for hd in range(heads):
-            m, l, acc = carry[hd]
-            o_s[d, :, hcols(hd)] = (acc / l).T.astype(jnp.bfloat16)
+            o_s[d, :, hcols(hd)] = (acc_buf[hd] / state[hd][1]).T.astype(jnp.bfloat16)
 
         @pl.when(d != 0)
         def _():
@@ -396,19 +422,25 @@
         @pl.when(d == 0)
         def _():
             o_own().start()
-
-    @pl.when(step == 4 * n - 1)
-    def _():
-        gather.finish()
-        o_own().wait()
-        for d in range(1, n):
-            src = lax.rem(me + d, n)
-            o_copy(d).wait_send()
-            pltpu.make_async_remote_copy(
-                src_ref=o_s.at[d], dst_ref=o_hbm.at[:, pl.ds(pl.multiple_of(src * cols, cols), cols)],
-                send_sem=o_send.at[d], recv_sem=o_recv.at[src], device_id=peer(d), device_id_type=MESH).wait_recv()
-            for chunk in range(2):
-                stats_copy(chunk, d).wait_send()
+        return carry
+
+    gather.relay()
+    lax.fori_loop(0, half, attend, 0)
+    gather.take((3, 7))
+    lax.fori_loop(half, n, attend, 0)
+    gather.finish()
+    o_own().wait()
+    for d in range(1, n):
+        src = lax.rem(me + d, n)
+        o_copy(d).wait_send()
+        pltpu.make_async_remote_copy(
+            src_ref=o_s.at[d], dst_ref=o_hbm.at[:, pl.ds(pl.multiple_of(src * cols, cols), cols)],
+            send_sem=o_send.at[d], recv_sem=o_recv.at[src], device_id=peer(d), device_id_type=MESH).wait_recv()
+        for chunk in range(2):
+            stats_copy(chunk, d).wait_send()
+    for i in range(n):
+        for which in range(2):
+            kv_store(which, i).wait()
 
 
 def block_call(n, h_full, wq, wk, wv, qg, kg, cos, sin, next_buf, cached):
@@ -416,57 +448,44 @@
     cols = wq.shape[1]
     tile = seq // n
     heads = cols // HEAD_DIM
-
-    def twice(i):
-        return (jnp.where(i < 2 * n, lax.rem(i, n), n - 1), 0)
-
-    def second(i):
-        return (jnp.clip(i - n, 0, n - 1), 0)
-
-    def third(i):
-        return (jnp.clip(i - 2 * n, 0, n - 1), 0)
-
-    def whole(i):
-        return (0, 0)
-
-    cache_tile = (tile, heads, HEAD_DIM) if cached else (tile, cols)
-    cache_shape = (seq,) + cache_tile[1:]
+    next_rows = next_buf.shape[0] // n
+    cache_tail = (heads, HEAD_DIM) if cached else (cols,)
     hbm = pl.BlockSpec(memory_space=pl.ANY)
-
-    def cache_map(index):
-        return (lambda i: index(i) + (0,)) if cached else index
-
+    vmem = pl.BlockSpec(memory_space=pltpu.VMEM)
     flops = 2 * seq * width * cols * 3 + 2 * seq * seq * cols * 2
+    cache = jax.ShapeDtypeStruct((seq,) + cache_tail, jnp.bfloat16)
     return pl.pallas_call(
         functools.partial(block_kernel, n, width),
-        grid=(4 * n,),
-        in_specs=[
-            pl.BlockSpec((tile, width), twice),
-            pl.BlockSpec((width, cols), whole), pl.BlockSpec((width, cols), whole), pl.BlockSpec((width, cols), whole),
-            pl.BlockSpec((1, cols), whole), pl.BlockSpec((1, cols), whole),
-            pl.BlockSpec((tile, HEAD_DIM), third), pl.BlockSpec((tile, HEAD_DIM), third),
-            hbm,
-        ],
-        out_specs=[
-            hbm, hbm,
-            pl.BlockSpec(cache_tile, cache_map(third)),
-            pl.BlockSpec(cache_tile, cache_map(second)),
-        ],
+        in_specs=[hbm, hbm, hbm, hbm, vmem, vmem, hbm, hbm, hbm],
+        out_specs=[hbm, hbm, hbm, hbm],
         out_shape=[
             jax.ShapeDtypeStruct((tile, n * cols), jnp.bfloat16),
             jax.ShapeDtypeStruct(next_buf.shape, next_buf.dtype),
-            jax.ShapeDtypeStruct(cache_shape, jnp.bfloat16),
-            jax.ShapeDtypeStruct(cache_shape, jnp.bfloat16),
+            cache, cache,
         ],
         input_output_aliases={8: 1},
         scratch_shapes=[
+            pltpu.VMEM((n, tile, width), jnp.bfloat16),
+            pltpu.VMEM((width, 2 * cols), jnp.bfloat16),
+            pltpu.VMEM((width, cols), jnp.bfloat16),
+            pltpu.VMEM((seq, HEAD_DIM), jnp.float32),
+            pltpu.VMEM((seq, HEAD_DIM), jnp.float32),
             pltpu.VMEM((n, tile, cols), jnp.bfloat16),
             pltpu.VMEM((n, tile, cols), jnp.bfloat16),
             pltpu.VMEM((n, cols, tile), jnp.bfloat16),
+            pltpu.VMEM((n, tile) + cache_tail, jnp.bfloat16),
+            pltpu.VMEM((n, tile) + cache_tail, jnp.bfloat16),
             pltpu.VMEM((n, n, 2 * tile // HEAD_DIM, HEAD_DIM), jnp.float32),
             pltpu.VMEM((n, tile, cols), jnp.bfloat16),
-            pltpu.VMEM((next_buf.shape[0] // n, width), jnp.bfloat16),
-            pltpu.VMEM((3, next_buf.shape[0] // n, width), jnp.bfloat16),
+            pltpu.VMEM((heads, tile, tile), jnp.float32),
+            pltpu.VMEM((heads, tile, tile), jnp.bfloat16),
+            pltpu.VMEM((heads, HEAD_DIM, tile), jnp.float32),
+            pltpu.VMEM((next_rows, width), jnp.bfloat16),
+            pltpu.VMEM((3, next_rows, width), jnp.bfloat16),
+            pltpu.SemaphoreType.DMA((n,)),
+            pltpu.SemaphoreType.DMA((3,)),
+            pltpu.SemaphoreType.DMA((2,)),
+            pltpu.SemaphoreType.DMA((2, n)),
             pltpu.SemaphoreType.DMA,
             pltpu.SemaphoreType.DMA((n, 2)),
             pltpu.SemaphoreType.DMA((n, 2)),
@@ -475,8 +494,7 @@
             pltpu.SemaphoreType.DMA,
         ] + GATHER_SEMS,
         compiler_params=pltpu.CompilerParams(
-            collective_id=1 if cached else 2, has_side_effects=True, vmem_limit_bytes=52 * 1024 * 1024,
-            dimension_semantics=('arbitrary',)),
+            collective_id=1 if cached else 2, has_side_effects=True, vmem_limit_bytes=62 * 1024 * 1024),
         cost_estimate=pl.CostEstimate(flops=flops, bytes_accessed=seq * width * 2 + 6 * seq * cols * 2, transcendentals=seq * seq * heads // 2),
         name='attn_block' if cached else 'attn_last',
     )(h_full, wq, wk, wv, qg, kg, cos, sin, next_buf)

time: 510 us -> 484 us (0.949)
  Pallas kernels: 499 us -> 482 us
  local copies, waits for them, and re-layouts: 7.77 us -> 0 us
    pallas_call x4, Pallas kernels: 388 us -> 372 us  [block_call(): pl.pallas_call(functools.partial(block_kernel, n, width), in_specs=[hbm,...]
    unnamed x16 -> x0, local copies, waits for them, and re-layouts: 7.77 us -> none
where the time goes in v3:
time: 484 us; the launch traced here: 483 us
  Pallas kernels  482 us (100%)
    pallas_call x4, Pallas kernels, block_call(): pl.pallas_call(functools.partial(block_kernel, n, width), in_specs=[hbm,...  372 us
    pallas_call x1, Pallas kernels, first_call(): pl.pallas_call(functools.partial(first_kernel, n, n_batch), in_specs=[hbm...  76.4 us
    pallas_call x1, Pallas kernels, last_call(): pl.pallas_call(functools.partial(last_kernel, n_batch), grid=(steps,), in...  34 us

profile of v3, /device:TPU:7, one launch (start us, length us, event | category | flops | bytes accessed | tf_op | source)
XLA Modules:
  0.0 483.4 jit_solution(10937850973438164805)
XLA Ops:
  0.6 0.6 maximum_bitcast_fusion.freq_ref
  1.2 76.4 %first_gather.1 = (bf16[4096,2048]{1,0:T(8,128)(2,1)}, bf16[4096,2048]{1,0:T(8,128)(2,1)}, bf16[4096,2048]{1,0:T(8,128)(2,1)}, bf16[4096,2048]{1,0:T(8,128)(2,1)...) custom-call(bf16[4,512,2048]{2,1,0:T(8,128)(2,1)} %refs_0_.1, f32[1,2048]{1,0:T(1,128)} %bitcast.5, ...), custom_call_target="tpu_custom_call" | custom-call | flops 100000000 | bytes 33554432 | tf_op jit(solution)/shard_map/first_gather/pallas_call | solution.py:194
  77.7 99.8 %attn_block.3 = (bf16[512,2048]{1,0:T(8,128)(2,1)}, bf16[4096,2048]{1,0:T(8,128)(2,1)}, bf16[4096,2,128]{2,1,0:T(2,128)(2,1)}, bf16[4096,2,128]{2,1,0:T(2,128)(2,1)}) custom-call(bf16[4096,2048]{1,0:T(8,128)(2,1)} %get-tuple-element.26.h_hbm, bf16[2048,256]{1,0:T(8,128)(2,1)} %wq_hbm.7, bf16[2048,256]{1,0:T(8,128)(2,1)} %wk_hbm.7, ...), custom_call_target="tpu_custom_call", output_to_operand_aliasing={{1}: (8, {})} | custom-call | flops 30064771072 | bytes 29360128 | tf_op jit(solution)/shard_map/attn_block/pallas_call | solution.py:457
  177.5 98.8 %attn_block.4 = (bf16[512,2048]{1,0:T(8,128)(2,1)}, bf16[4096,2048]{1,0:T(8,128)(2,1)}, bf16[4096,2,128]{2,1,0:T(2,128)(2,1)}, bf16[4096,2,128]{2,1,0:T(2,128)(2,1)}) custom-call(bf16[4096,2048]{1,0:T(8,128)(2,1)} %get-tuple-element.30.h_hbm, bf16[2048,256]{1,0:T(8,128)(2,1)} %wq_hbm.7, bf16[2048,256]{1,0:T(8,128)(2,1)} %wk_hbm.7, ...), custom_call_target="tpu_custom_call", output_to_operand_aliasing={{1}: (8, {})} | custom-call | flops 30064771072 | bytes 29360128 | tf_op jit(solution)/shard_map/attn_block/pallas_call | solution.py:457
  276.3 98.7 %attn_block.5 = (bf16[512,2048]{1,0:T(8,128)(2,1)}, bf16[4096,2048]{1,0:T(8,128)(2,1)}, bf16[4096,2,128]{2,1,0:T(2,128)(2,1)}, bf16[4096,2,128]{2,1,0:T(2,128)(2,1)}) custom-call(bf16[4096,2048]{1,0:T(8,128)(2,1)} %get-tuple-element.32.h_hbm, bf16[2048,256]{1,0:T(8,128)(2,1)} %wq_hbm.7, bf16[2048,256]{1,0:T(8,128)(2,1)} %wk_hbm.7, ...), custom_call_target="tpu_custom_call", output_to_operand_aliasing={{1}: (8, {})} | custom-call | flops 30064771072 | bytes 29360128 | tf_op jit(solution)/shard_map/attn_block/pallas_call | solution.py:457
  375.1 74.2 %attn_last.1 = (bf16[512,2048]{1,0:T(8,128)(2,1)}, bf16[2048,2048]{1,0:T(8,128)(2,1)}, bf16[4096,256]{1,0:T(8,128)(2,1)}, bf16[4096,256]{1,0:T(8,128)(2,1)}) custom-call(bf16[4096,2048]{1,0:T(8,128)(2,1)} %get-tuple-element.34.h_hbm, bf16[2048,256]{1,0:T(8,128)(2,1)} %wq_hbm.7, bf16[2048,256]{1,0:T(8,128)(2,1)} %wk_hbm.7, ...), custom_call_target="tpu_custom_call", output_to_operand_aliasing={{1}: (8, {})} | custom-call | flops 30064771072 | bytes 29360128 | tf_op jit(solution)/shard_map/attn_last/pallas_call | solution.py:457
  449.3 34.0 %last_proj.1 = (bf16[4,512,2048]{2,1,0:T(8,128)(2,1)}, bf16[4,4096,2,128]{3,2,1,0:T(2,128)(2,1)}, bf16[4,4096,2,128]{3,2,1,0:T(2,128)(2,1)}) custom-call(bf16[4,512,2048]{2,1,0:T(8,128)(2,1)} %refs_0_.1, bf16[2048,2048]{1,0:T(8,128)(2,1)} %get-tuple-element.36.refs_1_, bf16[512,2048]{1,0:T(8,128)(2,1)} %get-tuple-element.37.refs_2_, ...), custom_call_target="tpu_custom_call" | custom-call | flops 17179869184 | bytes 67108864 | tf_op jit(solution)/shard_map/last_proj/pallas_call | solution.py:602
  (1 shorter events, 0.0 us)

commit v4 on v3

--- a/solution.py
+++ b/solution.py
@@ -15,13 +15,13 @@
 
 FIRST = ((0, 2), (2, 1), (3, 1), (4, 4))
 SECOND = ((4, 2), (6, 1), (7, 1), (0, 4))
-PIECES = FIRST + SECOND + ((4, 4), (0, 4))
+PIECES = FIRST + SECOND + ((4, 2), (6, 2), (0, 2), (2, 2))
 LAST = len(PIECES)
 
 
 class RingGather:
     def __init__(self, buf, own, stage, me, ici_send, ici_recv, d2d_send, d2d_recv, keep):
-        self.buf, self.own, self.stage, self.me, self.rows = buf, own, stage, me, own.shape[0]
+        self.buf, self.own, self.stage, self.me, self.rows = buf, own, stage, me, stage.shape[1]
         self.ici_send, self.ici_recv, self.d2d_send, self.d2d_recv, self.keep = ici_send, ici_recv, d2d_send, d2d_recv, keep
         self.xn = me + 2 - 4 * lax.rem(me // 2, 2)
         self.yn = me + 4 - 8 * (me // 4)
@@ -51,16 +51,17 @@
     def copy(self, piece):
         first, rows = self.span(piece)
         if piece < 8:
-            src = self.own.at[pl.ds(first, rows)]
+            src = self.slot(self.me, piece) if self.own is None else self.own.at[pl.ds(first, rows)]
         else:
-            src = self.stage.at[1 if piece == 8 else 0, pl.ds(first, rows)]
+            src = self.stage.at[1 if piece < 10 else 0, pl.ds(first, rows)]
         return pltpu.make_async_remote_copy(
             src_ref=src, dst_ref=self.staged(piece), send_sem=self.ici_send.at[piece], recv_sem=self.ici_recv.at[piece],
-            device_id={'tp': self.xn if piece < 4 or piece == 8 else self.yn}, device_id_type=MESH)
+            device_id={'tp': self.xn if piece < 4 or piece in (8, 9) else self.yn}, device_id_type=MESH)
 
     def handover(self, piece):
         if piece == LAST:
-            src, dst = self.own, self.block(self.me)
+            dst = self.block(self.me)
+            src = dst if self.own is None else self.own
         else:
             src, dst = self.staged(piece), self.slot(self.source(piece), piece)
         return pltpu.make_async_remote_copy(
@@ -78,7 +79,7 @@
             self.handover(LAST).start()
 
     def relay(self):
-        for turns, onward in (((0, 1, 2), 9), ((4, 5, 6), 8)):
+        for turns, onward in (((0,), 10), ((4,), 8), ((1, 2), 11), ((5, 6), 9)):
             for piece in turns:
                 self.copy(piece).wait_recv()
             self.copy(onward).start()
@@ -95,7 +96,7 @@
             self.pass_on((piece,))
 
     def finish(self):
-        self.take((8, 9))
+        self.take((8, 10, 9, 11))
         for piece in range(LAST):
             self.copy(piece).wait_send()
             self.store(piece).wait()
@@ -218,19 +219,20 @@
 
 
 AHEAD = 2
+SPLIT = 2
 
 
 def block_kernel(n, width, h_hbm, wq_hbm, wk_hbm, wv_hbm, qg_ref, kg_ref, cos_hbm, sin_hbm, next_in,
                  o_hbm, next_buf, k_out, v_out,
-                 h_v, wqk_v, wv_v, cos_v, sin_v, q_s, k_s, vt_s, k_st, v_st, stats, o_s, s_buf, p_buf, acc_buf, own_v, stage,
-                 h_sem, w_sem, tab_sem, kv_sem, own_sem, st_send, st_recv, o_send, o_recv, o_local, *gather_sems):
+                 h_v, wqk_v, wv_v, cos_v, sin_v, q_s, k_s, vt_s, k_st, v_st, stats, o_s, s_buf, p_buf, acc_buf, stage,
+                 h_sem, w_sem, tab_sem, kv_sem, st_send, st_recv, o_send, o_recv, o_local, *gather_sems):
     me = lax.axis_index('tp')
     tile = h_v.shape[1]
     cols = wv_v.shape[1]
     heads = cols // HEAD_DIM
     groups = tile // HEAD_DIM
     half = n // 2
-    gather = RingGather(next_buf, own_v, stage, me, *gather_sems)
+    gather = RingGather(next_buf, None, stage, me, *gather_sems)
     scale = HEAD_DIM ** -0.5 * math.log2(math.e)
 
     def peer(d):
@@ -275,13 +277,10 @@
         pltpu.make_async_copy(wk_hbm, wqk_v.at[:, pl.ds(cols, cols)], w_sem.at[1]),
         pltpu.make_async_copy(wv_hbm, wv_v, w_sem.at[2])]
     tab_loads = [pltpu.make_async_copy(cos_hbm, cos_v, tab_sem.at[0]), pltpu.make_async_copy(sin_hbm, sin_v, tab_sem.at[1])]
-    own_load = pltpu.make_async_copy(gather.block(me), own_v, own_sem)
 
     greet(n, me)
-    own_load.start()
     for load in w_loads[:2] + [h_load(i) for i in range(AHEAD)] + w_loads[2:]:
         load.start()
-    own_load.wait()
     pl.semaphore_wait(pltpu.get_barrier_semaphore(), n - 1)
     gather.send((0,))
     for load in w_loads[:2]:
@@ -369,51 +368,64 @@
     nt = (((1,), (1,)), ((), ()))
     strip = 64
 
-    def softmax_step(j, hd, m, l):
+    span = tile // SPLIT
+    chains = [(hd, part) for hd in range(heads) for part in range(SPLIT)]
+
+    def softmax_step(j, chain, m, l):
+        hd, part = chain
+        qs = slice(part * span, (part + 1) * span)
         top = None
         for c in range(tile // strip):
-            part = jnp.max(s_buf[hd, c * strip:(c + 1) * strip, :].reshape(strip // 8, 8, tile), axis=0)
-            top = part if top is None else jnp.maximum(top, part)
+            best = jnp.max(s_buf[hd, c * strip:(c + 1) * strip, qs].reshape(strip // 8, 8, span), axis=0)
+            top = best if top is None else jnp.maximum(top, best)
         m_new = jnp.max(top, axis=0, keepdims=True)
         if m is not None:
             m_new = jnp.maximum(m, m_new)
         m_scaled = m_new * scale
         total = None
         for c in range(tile // strip):
-            p = jnp.exp2(s_buf[hd, c * strip:(c + 1) * strip, :] * scale - m_scaled)
-            part = jnp.sum(p.reshape(strip // 8, 8, tile), axis=0)
-            total = part if total is None else total + part
-            p_buf[hd, c * strip:(c + 1) * strip, :] = p.astype(jnp.bfloat16)
+            p = jnp.exp2(s_buf[hd, c * strip:(c + 1) * strip, qs] * scale - m_scaled)
+            add = jnp.sum(p.reshape(strip // 8, 8, span), axis=0)
+            total = add if total is None else total + add
+            p_buf[hd, c * strip:(c + 1) * strip, qs] = p.astype(jnp.bfloat16)
         l_new = jnp.sum(total, axis=0, keepdims=True)
-        pv = jnp.dot(vt_s[j, hcols(hd), :], p_buf[hd], preferred_element_type=jnp.float32)
+        pv = jnp.dot(vt_s[j, hcols(hd), :], p_buf[hd, :, qs], preferred_element_type=jnp.float32)
         if m is None:
-            acc_buf[hd] = pv
+            acc_buf[hd, :, qs] = pv
         else:
             alpha = jnp.exp2((m - m_new) * scale)
             l_new = l * alpha + l_new
-            acc_buf[hd] = acc_buf[hd] * alpha + pv
+            acc_buf[hd, :, qs] = acc_buf[hd, :, qs] * alpha + pv
         return m_new, l_new
 
     def attend(step, carry):
+        @pl.when(step == half)
+        def _():
+            gather.take((3, 7))
+
         d = lax.rem(step + 1, n)
         blk = lax.rem(me + d, n)
 
-        def scores(j, hd):
-            return lax.dot_general(k_s[j, :, hcols(hd)], q_s[blk, :, hcols(hd)], nt, preferred_element_type=jnp.float32)
-
-        keep = lax.broadcasted_iota(jnp.int32, (tile, tile), 0) <= lax.broadcasted_iota(jnp.int32, (tile, tile), 1)
-        for hd in range(heads):
-            s_buf[hd] = jnp.where(keep, scores(blk, hd), -jnp.inf)
-        state = tuple(softmax_step(blk, hd, None, None) for hd in range(heads))
+        def scores(j, chain):
+            hd, part = chain
+            return lax.dot_general(k_s[j, :, hcols(hd)], q_s[blk, part * span:(part + 1) * span, hcols(hd)], nt,
+                                   preferred_element_type=jnp.float32)
+
+        for hd, part in chains:
+            keep = (lax.broadcasted_iota(jnp.int32, (tile, span), 0)
+                    <= lax.broadcasted_iota(jnp.int32, (tile, span), 1) + part * span)
+            s_buf[hd, :, part * span:(part + 1) * span] = jnp.where(keep, scores(blk, (hd, part)), -jnp.inf)
+        state = tuple(softmax_step(blk, chain, None, None) for chain in chains)
 
         def body(j, state):
-            for hd in range(heads):
-                s_buf[hd] = scores(j, hd)
-            return tuple(softmax_step(j, hd, *state[hd]) for hd in range(heads))
+            for hd, part in chains:
+                s_buf[hd, :, part * span:(part + 1) * span] = scores(j, (hd, part))
+            return tuple(softmax_step(j, chain, *state[c]) for c, chain in enumerate(chains))
 
         state = lax.fori_loop(0, blk, body, state)
-        for hd in range(heads):
-            o_s[d, :, hcols(hd)] = (acc_buf[hd] / state[hd][1]).T.astype(jnp.bfloat16)
+        for c, (hd, part) in enumerate(chains):
+            qs = slice(part * span, (part + 1) * span)
+            o_s[d, qs, hcols(hd)] = (acc_buf[hd, :, qs] / state[c][1]).T.astype(jnp.bfloat16)
 
         @pl.when(d != 0)
         def _():
@@ -425,9 +437,7 @@
         return carry
 
     gather.relay()
-    lax.fori_loop(0, half, attend, 0)
-    gather.take((3, 7))
-    lax.fori_loop(half, n, attend, 0)
+    lax.fori_loop(0, n, attend, 0)
     gather.finish()
     o_own().wait()
     for d in range(1, n):
@@ -480,13 +490,11 @@
             pltpu.VMEM((heads, tile, tile), jnp.float32),
             pltpu.VMEM((heads, tile, tile), jnp.bfloat16),
             pltpu.VMEM((heads, HEAD_DIM, tile), jnp.float32),
-            pltpu.VMEM((next_rows, width), jnp.bfloat16),
             pltpu.VMEM((3, next_rows, width), jnp.bfloat16),
             pltpu.SemaphoreType.DMA((n,)),
             pltpu.SemaphoreType.DMA((3,)),
             pltpu.SemaphoreType.DMA((2,)),
             pltpu.SemaphoreType.DMA((2, n)),
-            pltpu.SemaphoreType.DMA,
             pltpu.SemaphoreType.DMA((n, 2)),
             pltpu.SemaphoreType.DMA((n, 2)),
             pltpu.SemaphoreType.DMA((n,)),

time: 484 us -> 480 us (level)
  no operation moved by 1% of the time
where the time goes in v4:
time: 480 us; the launch traced here: 479 us
  Pallas kernels  478 us (100%)
    pallas_call x4, Pallas kernels, block_call(): pl.pallas_call(functools.partial(block_kernel, n, width), in_specs=[hbm,...  369 us
    pallas_call x1, Pallas kernels, first_call(): pl.pallas_call(functools.partial(first_kernel, n, n_batch), in_specs=[hbm...  75 us
    pallas_call x1, Pallas kernels, last_call(): pl.pallas_call(functools.partial(last_kernel, n_batch), grid=(steps,), in...  34 us

profile of v4, /device:TPU:7, one launch (start us, length us, event | category | flops | bytes accessed | tf_op | source)
XLA Modules:
  0.0 479.0 jit_solution(12401761237248758699)
XLA Ops:
  0.6 0.6 maximum_bitcast_fusion.freq_ref
  1.2 75.0 %first_gather.1 = (bf16[4096,2048]{1,0:T(8,128)(2,1)}, bf16[4096,2048]{1,0:T(8,128)(2,1)}, bf16[4096,2048]{1,0:T(8,128)(2,1)}, bf16[4096,2048]{1,0:T(8,128)(2,1)...) custom-call(bf16[4,512,2048]{2,1,0:T(8,128)(2,1)} %refs_0_.1, f32[1,2048]{1,0:T(1,128)} %bitcast.5, ...), custom_call_target="tpu_custom_call" | custom-call | flops 100000000 | bytes 33554432 | tf_op jit(solution)/shard_map/first_gather/pallas_call | solution.py:195
  76.3 98.4 %attn_block.3 = (bf16[512,2048]{1,0:T(8,128)(2,1)}, bf16[4096,2048]{1,0:T(8,128)(2,1)}, bf16[4096,2,128]{2,1,0:T(2,128)(2,1)}, bf16[4096,2,128]{2,1,0:T(2,128)(2,1)}) custom-call(bf16[4096,2048]{1,0:T(8,128)(2,1)} %get-tuple-element.26.h_hbm, bf16[2048,256]{1,0:T(8,128)(2,1)} %wq_hbm.7, bf16[2048,256]{1,0:T(8,128)(2,1)} %wk_hbm.7, ...), custom_call_target="tpu_custom_call", output_to_operand_aliasing={{1}: (8, {})} | custom-call | flops 30064771072 | bytes 29360128 | tf_op jit(solution)/shard_map/attn_block/pallas_call | solution.py:467
  174.6 98.3 %attn_block.4 = (bf16[512,2048]{1,0:T(8,128)(2,1)}, bf16[4096,2048]{1,0:T(8,128)(2,1)}, bf16[4096,2,128]{2,1,0:T(2,128)(2,1)}, bf16[4096,2,128]{2,1,0:T(2,128)(2,1)}) custom-call(bf16[4096,2048]{1,0:T(8,128)(2,1)} %get-tuple-element.30.h_hbm, bf16[2048,256]{1,0:T(8,128)(2,1)} %wq_hbm.7, bf16[2048,256]{1,0:T(8,128)(2,1)} %wk_hbm.7, ...), custom_call_target="tpu_custom_call", output_to_operand_aliasing={{1}: (8, {})} | custom-call | flops 30064771072 | bytes 29360128 | tf_op jit(solution)/shard_map/attn_block/pallas_call | solution.py:467
  272.9 98.3 %attn_block.5 = (bf16[512,2048]{1,0:T(8,128)(2,1)}, bf16[4096,2048]{1,0:T(8,128)(2,1)}, bf16[4096,2,128]{2,1,0:T(2,128)(2,1)}, bf16[4096,2,128]{2,1,0:T(2,128)(2,1)}) custom-call(bf16[4096,2048]{1,0:T(8,128)(2,1)} %get-tuple-element.32.h_hbm, bf16[2048,256]{1,0:T(8,128)(2,1)} %wq_hbm.7, bf16[2048,256]{1,0:T(8,128)(2,1)} %wk_hbm.7, ...), custom_call_target="tpu_custom_call", output_to_operand_aliasing={{1}: (8, {})} | custom-call | flops 30064771072 | bytes 29360128 | tf_op jit(solution)/shard_map/attn_block/pallas_call | solution.py:467
  371.1 73.7 %attn_last.1 = (bf16[512,2048]{1,0:T(8,128)(2,1)}, bf16[2048,2048]{1,0:T(8,128)(2,1)}, bf16[4096,256]{1,0:T(8,128)(2,1)}, bf16[4096,256]{1,0:T(8,128)(2,1)}) custom-call(bf16[4096,2048]{1,0:T(8,128)(2,1)} %get-tuple-element.34.h_hbm, bf16[2048,256]{1,0:T(8,128)(2,1)} %wq_hbm.7, bf16[2048,256]{1,0:T(8,128)(2,1)} %wk_hbm.7, ...), custom_call_target="tpu_custom_call", output_to_operand_aliasing={{1}: (8, {})} | custom-call | flops 30064771072 | bytes 29360128 | tf_op jit(solution)/shard_map/attn_last/pallas_call | solution.py:467
  444.9 34.0 %last_proj.1 = (bf16[4,512,2048]{2,1,0:T(8,128)(2,1)}, bf16[4,4096,2,128]{3,2,1,0:T(2,128)(2,1)}, bf16[4,4096,2,128]{3,2,1,0:T(2,128)(2,1)}) custom-call(bf16[4,512,2048]{2,1,0:T(8,128)(2,1)} %refs_0_.1, bf16[2048,2048]{1,0:T(8,128)(2,1)} %get-tuple-element.36.refs_1_, bf16[512,2048]{1,0:T(8,128)(2,1)} %get-tuple-element.37.refs_2_, ...), custom_call_target="tpu_custom_call" | custom-call | flops 17179869184 | bytes 67108864 | tf_op jit(solution)/shard_map/last_proj/pallas_call | solution.py:610
  (1 shorter events, 0.0 us)

commit v5 on v4

--- a/solution.py
+++ b/solution.py
@@ -121,18 +121,22 @@
 
 def first_kernel(n, n_batch, x_hbm, gain_ref, wo_hbm, freq_ref,
                  h0, h1, h2, h3, wo_full, cos_hbm, sin_hbm,
-                 x_v, h_v, wo_v, stage, cos_v, sin_v, in_sem, wo_sem, out_sem, tab_sem, *gather_sems):
+                 x_v, h_v, wo_v, stage, cos_v, sin_v, in_sem, first_sem, wo_sem, out_sem, tab_sem, *gather_sems):
     me = lax.axis_index('tp')
     rows, width = x_v.shape[1:]
     wo_rows = wo_v.shape[0]
     hs = (h0, h1, h2, h3)
     greet(n, me)
-    loads = [pltpu.make_async_copy(x_hbm.at[b], x_v.at[b], in_sem.at[b]) for b in range(n_batch)]
+    loads = [pltpu.make_async_copy(x_hbm.at[b], x_v.at[b], in_sem.at[b]) for b in range(1, n_batch)]
     wo_load = pltpu.make_async_copy(wo_hbm, wo_v, wo_sem.at[0])
     wo_store = pltpu.make_async_copy(wo_v, wo_full.at[pl.ds(pl.multiple_of(me * wo_rows, wo_rows), wo_rows)], wo_sem.at[1])
     stores = [pltpu.make_async_copy(h_v.at[b], hs[b].at[pl.ds(pl.multiple_of(me * rows, rows), rows)], out_sem.at[b])
               for b in range(n_batch)]
-    loads[0].start()
+    fourth = rows // 4
+    first_loads = [pltpu.make_async_copy(x_hbm.at[0, pl.ds(q * fourth, fourth)], x_v.at[0, pl.ds(q * fourth, fourth)],
+                                         first_sem.at[q]) for q in range(4)]
+    for q in (0, 2, 1, 3):
+        first_loads[q].start()
 
     def norm(b, first=0, strips=rows // 64):
         def body(r, carry):
@@ -143,22 +147,26 @@
             return carry
         lax.fori_loop(first, first + strips, body, 0)
 
-    loads[0].wait()
-    for load in loads[1:]:
-        load.start()
-    wo_load.start()
     quarter = rows // 256
-    norm(0, 0, quarter)
-    norm(0, 2 * quarter, quarter)
+
+    def norm_first(q):
+        first_loads[q].wait()
+        norm(0, q * quarter, quarter)
+
+    norm_first(0)
+    norm_first(2)
     pl.semaphore_wait(pltpu.get_barrier_semaphore(), n - 1)
     gather = RingGather(h0, h_v.at[0], stage, me, *gather_sems)
     gather.send((0,))
-    norm(0, quarter, quarter)
-    norm(0, 3 * quarter, quarter)
+    norm_first(1)
+    norm_first(3)
     gather.send((1, 2, 3))
+    for load in loads:
+        load.start()
+    wo_load.start()
     stores[0].start()
     for b in range(1, n_batch):
-        loads[b].wait()
+        loads[b - 1].wait()
         norm(b)
         stores[b].start()
     wo_load.wait()
@@ -207,6 +215,7 @@
             pltpu.VMEM((seq, HEAD_DIM), jnp.float32),
             pltpu.VMEM((seq, HEAD_DIM), jnp.float32),
             pltpu.SemaphoreType.DMA((n_batch,)),
+            pltpu.SemaphoreType.DMA((4,)),
             pltpu.SemaphoreType.DMA((2,)),
             pltpu.SemaphoreType.DMA((n_batch,)),
             pltpu.SemaphoreType.DMA((2,)),
@@ -218,7 +227,7 @@
     )(x_local, gain, wo_rows, freq)
 
 
-AHEAD = 2
+AHEAD = 3
 SPLIT = 2
 
 
@@ -371,11 +380,11 @@
     span = tile // SPLIT
     chains = [(hd, part) for hd in range(heads) for part in range(SPLIT)]
 
-    def softmax_step(j, chain, m, l):
+    def softmax_step(j, chain, m, l, keys):
         hd, part = chain
         qs = slice(part * span, (part + 1) * span)
         top = None
-        for c in range(tile // strip):
+        for c in range(keys // strip):
             best = jnp.max(s_buf[hd, c * strip:(c + 1) * strip, qs].reshape(strip // 8, 8, span), axis=0)
             top = best if top is None else jnp.maximum(top, best)
         m_new = jnp.max(top, axis=0, keepdims=True)
@@ -383,13 +392,13 @@
             m_new = jnp.maximum(m, m_new)
         m_scaled = m_new * scale
         total = None
-        for c in range(tile // strip):
+        for c in range(keys // strip):
             p = jnp.exp2(s_buf[hd, c * strip:(c + 1) * strip, qs] * scale - m_scaled)
             add = jnp.sum(p.reshape(strip // 8, 8, span), axis=0)
             total = add if total is None else total + add
             p_buf[hd, c * strip:(c + 1) * strip, qs] = p.astype(jnp.bfloat16)
         l_new = jnp.sum(total, axis=0, keepdims=True)
-        pv = jnp.dot(vt_s[j, hcols(hd), :], p_buf[hd, :, qs], preferred_element_type=jnp.float32)
+        pv = jnp.dot(vt_s[j, hcols(hd), :keys], p_buf[hd, :keys, qs], preferred_element_type=jnp.float32)
         if m is None:
             acc_buf[hd, :, qs] = pv
         else:
@@ -406,21 +415,22 @@
         d = lax.rem(step + 1, n)
         blk = lax.rem(me + d, n)
 
-        def scores(j, chain):
+        def scores(j, chain, keys=tile):
             hd, part = chain
-            return lax.dot_general(k_s[j, :, hcols(hd)], q_s[blk, part * span:(part + 1) * span, hcols(hd)], nt,
+            return lax.dot_general(k_s[j, :keys, hcols(hd)], q_s[blk, part * span:(part + 1) * span, hcols(hd)], nt,
                                    preferred_element_type=jnp.float32)
 
         for hd, part in chains:
-            keep = (lax.broadcasted_iota(jnp.int32, (tile, span), 0)
-                    <= lax.broadcasted_iota(jnp.int32, (tile, span), 1) + part * span)
-            s_buf[hd, :, part * span:(part + 1) * span] = jnp.where(keep, scores(blk, (hd, part)), -jnp.inf)
-        state = tuple(softmax_step(blk, chain, None, None) for chain in chains)
+            keys = (part + 1) * span
+            keep = (lax.broadcasted_iota(jnp.int32, (keys, span), 0)
+                    <= lax.broadcasted_iota(jnp.int32, (keys, span), 1) + part * span)
+            s_buf[hd, :keys, part * span:keys] = jnp.where(keep, scores(blk, (hd, part), keys), -jnp.inf)
+        state = tuple(softmax_step(blk, chain, None, None, (chain[1] + 1) * span) for chain in chains)
 
         def body(j, state):
             for hd, part in chains:
                 s_buf[hd, :, part * span:(part + 1) * span] = scores(j, (hd, part))
-            return tuple(softmax_step(j, chain, *state[c]) for c, chain in enumerate(chains))
+            return tuple(softmax_step(j, chain, *state[c], tile) for c, chain in enumerate(chains))
 
         state = lax.fori_loop(0, blk, body, state)
         for c, (hd, part) in enumerate(chains):

time: 480 us -> 479 us (level)
  no operation moved by 1% of the time
where the time goes in v5:
time: 479 us; the launch traced here: 478 us
  Pallas kernels  477 us (100%)
    pallas_call x4, Pallas kernels, block_call(): pl.pallas_call(functools.partial(block_kernel, n, width), in_specs=[hbm,...  369 us
    pallas_call x1, Pallas kernels, first_call(): pl.pallas_call(functools.partial(first_kernel, n, n_batch), in_specs=[hbm...  74.6 us
    pallas_call x1, Pallas kernels, last_call(): pl.pallas_call(functools.partial(last_kernel, n_batch), grid=(steps,), in...  34 us

profile of v5, /device:TPU:7, one launch (start us, length us, event | category | flops | bytes accessed | tf_op | source)
XLA Modules:
  0.0 478.5 jit_solution(9266958780176445269)
XLA Ops:
  0.6 0.6 maximum_bitcast_fusion.freq_ref
  1.2 74.6 %first_gather.1 = (bf16[4096,2048]{1,0:T(8,128)(2,1)}, bf16[4096,2048]{1,0:T(8,128)(2,1)}, bf16[4096,2048]{1,0:T(8,128)(2,1)}, bf16[4096,2048]{1,0:T(8,128)(2,1)...) custom-call(bf16[4,512,2048]{2,1,0:T(8,128)(2,1)} %refs_0_.1, f32[1,2048]{1,0:T(1,128)} %bitcast.5, ...), custom_call_target="tpu_custom_call" | custom-call | flops 100000000 | bytes 33554432 | tf_op jit(solution)/shard_map/first_gather/pallas_call | solution.py:203
  75.8 98.3 %attn_block.3 = (bf16[512,2048]{1,0:T(8,128)(2,1)}, bf16[4096,2048]{1,0:T(8,128)(2,1)}, bf16[4096,2,128]{2,1,0:T(2,128)(2,1)}, bf16[4096,2,128]{2,1,0:T(2,128)(2,1)}) custom-call(bf16[4096,2048]{1,0:T(8,128)(2,1)} %get-tuple-element.26.h_hbm, bf16[2048,256]{1,0:T(8,128)(2,1)} %wq_hbm.7, bf16[2048,256]{1,0:T(8,128)(2,1)} %wk_hbm.7, ...), custom_call_target="tpu_custom_call", output_to_operand_aliasing={{1}: (8, {})} | custom-call | flops 30064771072 | bytes 29360128 | tf_op jit(solution)/shard_map/attn_block/pallas_call | solution.py:477
  174.2 98.3 %attn_block.4 = (bf16[512,2048]{1,0:T(8,128)(2,1)}, bf16[4096,2048]{1,0:T(8,128)(2,1)}, bf16[4096,2,128]{2,1,0:T(2,128)(2,1)}, bf16[4096,2,128]{2,1,0:T(2,128)(2,1)}) custom-call(bf16[4096,2048]{1,0:T(8,128)(2,1)} %get-tuple-element.30.h_hbm, bf16[2048,256]{1,0:T(8,128)(2,1)} %wq_hbm.7, bf16[2048,256]{1,0:T(8,128)(2,1)} %wk_hbm.7, ...), custom_call_target="tpu_custom_call", output_to_operand_aliasing={{1}: (8, {})} | custom-call | flops 30064771072 | bytes 29360128 | tf_op jit(solution)/shard_map/attn_block/pallas_call | solution.py:477
  272.4 98.3 %attn_block.5 = (bf16[512,2048]{1,0:T(8,128)(2,1)}, bf16[4096,2048]{1,0:T(8,128)(2,1)}, bf16[4096,2,128]{2,1,0:T(2,128)(2,1)}, bf16[4096,2,128]{2,1,0:T(2,128)(2,1)}) custom-call(bf16[4096,2048]{1,0:T(8,128)(2,1)} %get-tuple-element.32.h_hbm, bf16[2048,256]{1,0:T(8,128)(2,1)} %wq_hbm.7, bf16[2048,256]{1,0:T(8,128)(2,1)} %wk_hbm.7, ...), custom_call_target="tpu_custom_call", output_to_operand_aliasing={{1}: (8, {})} | custom-call | flops 30064771072 | bytes 29360128 | tf_op jit(solution)/shard_map/attn_block/pallas_call | solution.py:477
  370.7 73.7 %attn_last.1 = (bf16[512,2048]{1,0:T(8,128)(2,1)}, bf16[2048,2048]{1,0:T(8,128)(2,1)}, bf16[4096,256]{1,0:T(8,128)(2,1)}, bf16[4096,256]{1,0:T(8,128)(2,1)}) custom-call(bf16[4096,2048]{1,0:T(8,128)(2,1)} %get-tuple-element.34.h_hbm, bf16[2048,256]{1,0:T(8,128)(2,1)} %wq_hbm.7, bf16[2048,256]{1,0:T(8,128)(2,1)} %wk_hbm.7, ...), custom_call_target="tpu_custom_call", output_to_operand_aliasing={{1}: (8, {})} | custom-call | flops 30064771072 | bytes 29360128 | tf_op jit(solution)/shard_map/attn_last/pallas_call | solution.py:477
  444.4 34.0 %last_proj.1 = (bf16[4,512,2048]{2,1,0:T(8,128)(2,1)}, bf16[4,4096,2,128]{3,2,1,0:T(2,128)(2,1)}, bf16[4,4096,2,128]{3,2,1,0:T(2,128)(2,1)}) custom-call(bf16[4,512,2048]{2,1,0:T(8,128)(2,1)} %refs_0_.1, bf16[2048,2048]{1,0:T(8,128)(2,1)} %get-tuple-element.36.refs_1_, bf16[512,2048]{1,0:T(8,128)(2,1)} %get-tuple-element.37.refs_2_, ...), custom_call_target="tpu_custom_call" | custom-call | flops 17179869184 | bytes 67108864 | tf_op jit(solution)/shard_map/last_proj/pallas_call | solution.py:620
  (1 shorter events, 0.0 us)

commit v6 on v5

--- a/solution.py
+++ b/solution.py
@@ -518,7 +518,7 @@
     )(h_full, wq, wk, wv, qg, kg, cos, sin, next_buf)
 
 
-N_CHUNK = 4
+N_CHUNK = 8
 
 
 def last_kernel(n_batch, *refs):

time: 479 us -> 488 us (1.019)
  Pallas kernels: 477 us -> 486 us
    pallas_call x1, Pallas kernels: 34 us -> 42.5 us  [last_call(): pl.pallas_call(functools.partial(last_kernel, n_batch), grid=(steps,), in...]
where the time goes in v6:
time: 488 us; the launch traced here: 487 us
  Pallas kernels  486 us (100%)
    pallas_call x4, Pallas kernels, block_call(): pl.pallas_call(functools.partial(block_kernel, n, width), in_specs=[hbm,...  369 us
    pallas_call x1, Pallas kernels, first_call(): pl.pallas_call(functools.partial(first_kernel, n, n_batch), in_specs=[hbm...  74.6 us
    pallas_call x1, Pallas kernels, last_call(): pl.pallas_call(functools.partial(last_kernel, n_batch), grid=(steps,), in...  42.5 us

profile of v6, /device:TPU:7, one launch (start us, length us, event | category | flops | bytes accessed | tf_op | source)
XLA Modules:
  0.0 487.1 jit_solution(18210101838947431774)
XLA Ops:
  0.6 0.6 maximum_bitcast_fusion.freq_ref
  1.2 74.6 %first_gather.1 = (bf16[4096,2048]{1,0:T(8,128)(2,1)}, bf16[4096,2048]{1,0:T(8,128)(2,1)}, bf16[4096,2048]{1,0:T(8,128)(2,1)}, bf16[4096,2048]{1,0:T(8,128)(2,1)...) custom-call(bf16[4,512,2048]{2,1,0:T(8,128)(2,1)} %refs_0_.1, f32[1,2048]{1,0:T(1,128)} %bitcast.5, ...), custom_call_target="tpu_custom_call" | custom-call | flops 100000000 | bytes 33554432 | tf_op jit(solution)/shard_map/first_gather/pallas_call | solution.py:203
  75.8 98.3 %attn_block.3 = (bf16[512,2048]{1,0:T(8,128)(2,1)}, bf16[4096,2048]{1,0:T(8,128)(2,1)}, bf16[4096,2,128]{2,1,0:T(2,128)(2,1)}, bf16[4096,2,128]{2,1,0:T(2,128)(2,1)}) custom-call(bf16[4096,2048]{1,0:T(8,128)(2,1)} %get-tuple-element.26.h_hbm, bf16[2048,256]{1,0:T(8,128)(2,1)} %wq_hbm.7, bf16[2048,256]{1,0:T(8,128)(2,1)} %wk_hbm.7, ...), custom_call_target="tpu_custom_call", output_to_operand_aliasing={{1}: (8, {})} | custom-call | flops 30064771072 | bytes 29360128 | tf_op jit(solution)/shard_map/attn_block/pallas_call | solution.py:477
  174.2 98.3 %attn_block.4 = (bf16[512,2048]{1,0:T(8,128)(2,1)}, bf16[4096,2048]{1,0:T(8,128)(2,1)}, bf16[4096,2,128]{2,1,0:T(2,128)(2,1)}, bf16[4096,2,128]{2,1,0:T(2,128)(2,1)}) custom-call(bf16[4096,2048]{1,0:T(8,128)(2,1)} %get-tuple-element.30.h_hbm, bf16[2048,256]{1,0:T(8,128)(2,1)} %wq_hbm.7, bf16[2048,256]{1,0:T(8,128)(2,1)} %wk_hbm.7, ...), custom_call_target="tpu_custom_call", output_to_operand_aliasing={{1}: (8, {})} | custom-call | flops 30064771072 | bytes 29360128 | tf_op jit(solution)/shard_map/attn_block/pallas_call | solution.py:477
  272.4 98.3 %attn_block.5 = (bf16[512,2048]{1,0:T(8,128)(2,1)}, bf16[4096,2048]{1,0:T(8,128)(2,1)}, bf16[4096,2,128]{2,1,0:T(2,128)(2,1)}, bf16[4096,2,128]{2,1,0:T(2,128)(2,1)}) custom-call(bf16[4096,2048]{1,0:T(8,128)(2,1)} %get-tuple-element.32.h_hbm, bf16[2048,256]{1,0:T(8,128)(2,1)} %wq_hbm.7, bf16[2048,256]{1,0:T(8,128)(2,1)} %wk_hbm.7, ...), custom_call_target="tpu_custom_call", output_to_operand_aliasing={{1}: (8, {})} | custom-call | flops 30064771072 | bytes 29360128 | tf_op jit(solution)/shard_map/attn_block/pallas_call | solution.py:477
  370.7 73.7 %attn_last.1 = (bf16[512,2048]{1,0:T(8,128)(2,1)}, bf16[2048,2048]{1,0:T(8,128)(2,1)}, bf16[4096,256]{1,0:T(8,128)(2,1)}, bf16[4096,256]{1,0:T(8,128)(2,1)}) custom-call(bf16[4096,2048]{1,0:T(8,128)(2,1)} %get-tuple-element.34.h_hbm, bf16[2048,256]{1,0:T(8,128)(2,1)} %wq_hbm.7, bf16[2048,256]{1,0:T(8,128)(2,1)} %wk_hbm.7, ...), custom_call_target="tpu_custom_call", output_to_operand_aliasing={{1}: (8, {})} | custom-call | flops 30064771072 | bytes 29360128 | tf_op jit(solution)/shard_map/attn_last/pallas_call | solution.py:477
  444.4 42.5 %last_proj.1 = (bf16[4,512,2048]{2,1,0:T(8,128)(2,1)}, bf16[4,4096,2,128]{3,2,1,0:T(2,128)(2,1)}, bf16[4,4096,2,128]{3,2,1,0:T(2,128)(2,1)}) custom-call(bf16[4,512,2048]{2,1,0:T(8,128)(2,1)} %refs_0_.1, bf16[2048,2048]{1,0:T(8,128)(2,1)} %get-tuple-element.36.refs_1_, bf16[512,2048]{1,0:T(8,128)(2,1)} %get-tuple-element.37.refs_2_, ...), custom_call_target="tpu_custom_call" | custom-call | flops 17179869184 | bytes 67108864 | tf_op jit(solution)/shard_map/last_proj/pallas_call | solution.py:620
  (1 shorter events, 0.0 us)
